TPU v7x, 256 devices: a whole 4x4x8 slice. The times are simulated.
256 devices in a mesh: gx: 4 (over y), gy: 8 (over z), gz: 8 (over x, core).
Axes of the slice: x: 4, y: 4, z: 8, core: 2. Of those that a mesh axis runs over, the one named last changes fastest.
Arguments:
- descriptors: float32 [64, 2097152], P(None, ('gx', 'gy', 'gz')), may hold values from -6 to 6
- types: int32 [2097152], P(('gx', 'gy', 'gz')), may hold values from 0 to 2
- offsets: float32 [3, 2097152], P(None, ('gx', 'gy', 'gz')), may hold values from 0 to 1
- stencil_base: int32 [3, 2097152], P(None, ('gx', 'gy', 'gz')), may hold values from 0 to 47, as said below
- w_first: float32 [3, 25, 64], replicated, may hold values from -0.75 to 0.75
- w_second: float32 [3, 25, 25], replicated, may hold values from -1.25 to 1.25
- w_out: float32 [3, 25], replicated, may hold values from -1.25 to 1.25
- hardness: float32 [3], replicated, may hold values from 0.5 to 3
- sr_first: float32 [3, 25, 64], replicated, may hold values from -0.75 to 0.75
- sr_charge: float32 [3, 25], replicated, may hold values from -6 to 6
- sr_out: float32 [3, 25], replicated, may hold values from -1.25 to 1.25
Outputs:
- charges: float32 [2097152], P(('gx', 'gy', 'gz'))
- forces: float32 [3, 2097152], P(None, ('gx', 'gy', 'gz'))
- short_energy: float32 [2097152], P(('gx', 'gy', 'gz'))
Inputs may be any that keep to these rules, and one draw needn't show every extreme that they name: stencil_base[d, a] is a cell of the atom's brick: below 48, 24 and 24 for d = 0, 1, 2.
All inputs are finite; a program needn't handle non-finite values.
Results may differ from a plain program's by a relative error of at most 0.0003.
Values sent between devices are 32-bit elements; how exact they have to be, the bound alone decides.
A program may use at most 320 MiB of HBM per device.

v0:
```python
import math

import jax
import jax.numpy as jnp
from jax import lax
from jax.sharding import Mesh
from jax.sharding import PartitionSpec as P

M = 192
ITERS = 2
GX_GZ = ("gx", "gz_0", "gz_1")
GZ = ("gz_0", "gz_1")
GX_GY_GZ = ("gx", "gy", "gz_0", "gz_1")


smear = 0.75


def by_axis(array, axes):
    for axis in axes:
        array = lax.psum(array, axis)
    return array


def with_halo(cells, sides, width):
    for axis, dim in sides:
        count = lax.axis_size(axis)
        head = lax.slice_in_dim(cells, 0, width, axis=dim)
        tail = lax.slice_in_dim(cells, cells.shape[dim] - width, cells.shape[dim], axis=dim)
        cells = jnp.concatenate(
            [
                lax.ppermute(tail, axis, [(i, (i + 1) % count) for i in range(count)]),
                cells,
                lax.ppermute(head, axis, [((i + 1) % count, i) for i in range(count)]),
            ],
            axis=dim,
        )
    return cells


def cardinal(order, offset):
    if order == 2:
        return jnp.maximum(1.0 - jnp.abs(offset - 1.0), 0.0)
    return (
        offset * cardinal(order - 1, offset) + (order - offset) * cardinal(order - 1, offset - 1.0)
    ) / (order - 1)


def spline_tables(offsets):
    weights = jnp.stack([cardinal(5, offsets + 4.0 - point) for point in range(5)], axis=1)
    slopes = jnp.stack(
        [
            cardinal(4, offsets + 4.0 - point) - cardinal(4, offsets + 3.0 - point)
            for point in range(5)
        ],
        axis=1,
    )
    return (weights, slopes)


def signed_freq(number, length):
    return jnp.where(2 * number >= length, number - length, number).astype(jnp.float32)


def element_net(first, second, final, descriptors, onehot):
    hidden = jnp.tanh(
        jnp.einsum("ehf,fa->eha", first, descriptors, precision=lax.Precision.HIGHEST)
    )
    hidden = jnp.tanh(jnp.einsum("ehg,ega->eha", second, hidden, precision=lax.Precision.HIGHEST))
    output = jnp.einsum("eh,eha->ea", final, hidden, precision=lax.Precision.HIGHEST)
    return jnp.sum(onehot * output, axis=0)


def dft_tables(length):
    ramp_cells = jnp.arange(length, dtype=jnp.int32)
    angle = (
        2.0
        * math.pi
        / length
        * (ramp_cells[:, None] * ramp_cells[None, :] % length).astype(jnp.float32)
    )
    return (jnp.cos(angle), jnp.sin(angle))


def along(values, matrix, dim):
    letters = "abc"
    target = letters[:dim] + "k" + letters[dim + 1 :]
    return jnp.einsum(
        letters + "," + letters[dim] + "k->" + target,
        values,
        matrix,
        precision=lax.Precision.HIGHEST,
    )


def forward(real_part, imag_part, cosine, sine, dim):
    return (
        along(real_part, cosine, dim) + along(imag_part, sine, dim),
        along(imag_part, cosine, dim) - along(real_part, sine, dim),
    )


def backward(real_part, imag_part, cosine, sine, dim):
    return (
        along(real_part, cosine, dim) - along(imag_part, sine, dim),
        along(imag_part, cosine, dim) + along(real_part, sine, dim),
    )


def green_block(second_len, third_freq):
    first_freq = signed_freq(jnp.arange(M, dtype=jnp.int32), M)
    second_freq = signed_freq(
        lax.axis_index(GX_GZ) * second_len + jnp.arange(second_len, dtype=jnp.int32), M
    )
    factor = 2.0 * math.pi / M
    wave = (
        factor
        * factor
        * (
            first_freq[:, None, None] ** 2
            + second_freq[None, :, None] ** 2
            + third_freq[None, None, :] ** 2
        )
    )
    safe = jnp.where(wave > 0, wave, 1.0)
    green = jnp.where(wave > 0, 4.0 * math.pi * jnp.exp(-0.5 * smear * smear * wave) / safe, 0.0)
    return green * (1.0 / (M * M * M))


def spectral(density, cosine, sine):
    columns = lax.all_to_all(density, GZ, split_axis=0, concat_axis=2, tiled=True)
    real_part = along(columns, cosine, 2)
    imag_part = -along(columns, sine, 2)
    real_part, imag_part = (
        lax.all_to_all(real_part, "gy", split_axis=2, concat_axis=1, tiled=True),
        lax.all_to_all(imag_part, "gy", split_axis=2, concat_axis=1, tiled=True),
    )
    real_part, imag_part = forward(real_part, imag_part, cosine, sine, 1)
    real_part, imag_part = (
        lax.all_to_all(real_part, GX_GZ, split_axis=1, concat_axis=0, tiled=True),
        lax.all_to_all(imag_part, GX_GZ, split_axis=1, concat_axis=0, tiled=True),
    )
    real_part, imag_part = forward(real_part, imag_part, cosine, sine, 0)
    third_len = real_part.shape[2]
    third_freq = signed_freq(
        lax.axis_index("gy") * third_len + jnp.arange(third_len, dtype=jnp.int32), M
    )
    kernel = green_block(real_part.shape[1], third_freq)
    real_part, imag_part = backward(real_part * kernel, imag_part * kernel, cosine, sine, 0)
    real_part, imag_part = (
        lax.all_to_all(real_part, GX_GZ, split_axis=0, concat_axis=1, tiled=True),
        lax.all_to_all(imag_part, GX_GZ, split_axis=0, concat_axis=1, tiled=True),
    )
    real_part, imag_part = backward(real_part, imag_part, cosine, sine, 1)
    real_part, imag_part = (
        lax.all_to_all(real_part, "gy", split_axis=1, concat_axis=2, tiled=True),
        lax.all_to_all(imag_part, "gy", split_axis=1, concat_axis=2, tiled=True),
    )
    potential = along(real_part, cosine, 2) - along(imag_part, sine, 2)
    return lax.all_to_all(potential, GZ, split_axis=2, concat_axis=0, tiled=True)


def fold_rims(extended, dim, length):
    core = lax.slice_in_dim(extended, 4, length + 4, axis=dim)
    lower = lax.slice_in_dim(extended, 0, 2, axis=dim)
    upper = lax.slice_in_dim(extended, length + 6, length + 8, axis=dim)
    lower_pad = [(0, 0), (0, 0), (0, 0)]
    upper_pad = [(0, 0), (0, 0), (0, 0)]
    lower_pad[dim] = (0, length - 2)
    upper_pad[dim] = (length - 2, 0)
    return core + jnp.pad(lower, lower_pad) + jnp.pad(upper, upper_pad)


def cell_masks(spline_rows, base_cells, ext_len):
    ramp_cells = jnp.arange(ext_len, dtype=jnp.int32)[:, None]
    result = jnp.zeros((ext_len, base_cells.shape[0]), jnp.float32)
    for point in range(5):
        result = result + jnp.where(
            ramp_cells == base_cells[None, :] + point, spline_rows[point][None, :], 0.0
        )
    return result


def spread_local(first_mask, second_mask, third_mask):
    paired = (first_mask[:, None, :] * second_mask[None, :, :]).reshape(-1, first_mask.shape[1])
    grid = jnp.dot(paired, third_mask.T, precision=lax.Precision.HIGHEST)
    return grid.reshape(first_mask.shape[0], second_mask.shape[0], third_mask.shape[0])


def third_contract(extended, third_mask):
    flat_rows = extended.reshape(-1, extended.shape[2])
    inner = jnp.dot(flat_rows, third_mask, precision=lax.Precision.HIGHEST)
    return inner.reshape(extended.shape[0], extended.shape[1], third_mask.shape[1])


def outer_contract(inner, first_mask, second_mask):
    partial_rows = jnp.sum(inner * second_mask[None, :, :], axis=1)
    return jnp.sum(partial_rows * first_mask, axis=0)


def square_sum(residual):
    return by_axis(jnp.sum(residual * residual), GX_GY_GZ)


def per_device(
    descriptors,
    types,
    offsets,
    stencil_base,
    w_first,
    w_second,
    w_out,
    hardness,
    sr_first,
    sr_charge,
    sr_out,
):
    elements = w_first.shape[0]
    onehot = (types[None, :] == jnp.arange(elements, dtype=jnp.int32)[:, None]).astype(jnp.float32)
    chi = element_net(w_first, w_second, w_out, descriptors, onehot)
    atom_hardness = jnp.sum(onehot * hardness[:, None], axis=0)
    weights, slopes = spline_tables(offsets)
    brick_first = M // lax.axis_size("gx")
    brick_second = M // lax.axis_size("gy")
    brick_third = M // lax.axis_size(GZ)
    first_weight = cell_masks(weights[0], stencil_base[0], brick_first + 4)
    second_weight = cell_masks(weights[1], stencil_base[1], brick_second + 4)
    third_weight = cell_masks(weights[2], stencil_base[2], brick_third + 4)
    first_slope = cell_masks(slopes[0], stencil_base[0], brick_first + 4)
    second_slope = cell_masks(slopes[1], stencil_base[1], brick_second + 4)
    third_slope = cell_masks(slopes[2], stencil_base[2], brick_third + 4)
    cosine, sine = dft_tables(M)
    total_atoms = float(descriptors.shape[1] * lax.axis_size(GX_GY_GZ))
    chi_total = by_axis(jnp.sum(chi), GX_GY_GZ)
    residual = chi_total / total_atoms - chi
    norm_now = square_sum(residual)
    direction = residual
    charges = jnp.zeros_like(chi)
    history = []
    for iteration in range(ITERS):
        grid = spread_local(first_weight * direction[None, :], second_weight, third_weight)
        rims = with_halo(grid, (("gx", 0), ("gy", 1), (GZ, 2)), 2)
        density = fold_rims(rims, 0, brick_first)
        density = fold_rims(density, 1, brick_second)
        density = fold_rims(density, 2, brick_third)
        potential = spectral(density, cosine, sine)
        extended = with_halo(potential, (("gx", 0), ("gy", 1), (GZ, 2)), 2)
        inner = third_contract(extended, third_weight)
        image = atom_hardness * direction + outer_contract(inner, first_weight, second_weight)
        curvature, image_total = (
            by_axis(jnp.sum(direction * image), GX_GY_GZ),
            by_axis(jnp.sum(image), GX_GY_GZ),
        )
        step_size = norm_now / curvature
        charges = charges + step_size * direction
        residual = residual - step_size * (image - image_total / total_atoms)
        if iteration + 1 < ITERS:
            norm_next = square_sum(residual)
        history.append((step_size, extended))
        if iteration + 1 < ITERS:
            direction = residual + norm_next / norm_now * direction
            norm_now = norm_next
    final_grid = history[0][0] * history[0][1]
    for step_size, extended in history[1:]:
        final_grid = final_grid + step_size * extended
    inner_weight = third_contract(final_grid, third_weight)
    inner_slope = third_contract(final_grid, third_slope)
    forces = -charges[None, :] * jnp.stack(
        [
            outer_contract(inner_weight, first_slope, second_weight),
            outer_contract(inner_weight, first_weight, second_slope),
            outer_contract(inner_slope, first_weight, second_weight),
        ]
    )
    hidden = jnp.tanh(
        jnp.einsum("ehf,fa->eha", sr_first, descriptors, precision=lax.Precision.HIGHEST)
        + sr_charge[:, :, None] * charges[None, None, :]
    )
    short_energy = jnp.sum(
        onehot * jnp.einsum("eh,eha->ea", sr_out, hidden, precision=lax.Precision.HIGHEST), axis=0
    )
    return (charges, forces, short_energy)


def solution(mesh):
    torus = Mesh(
        mesh.devices.reshape(mesh.shape["gx"], mesh.shape["gy"], 4, 2), ("gx", "gy", "gz_0", "gz_1")
    )
    placed = (
        P(None, GX_GY_GZ),
        P(GX_GY_GZ),
        P(None, GX_GY_GZ),
        P(None, GX_GY_GZ),
        P(),
        P(),
        P(),
        P(),
        P(),
        P(),
        P(),
    )
    return jax.shard_map(
        per_device,
        mesh=torus,
        in_specs=placed,
        out_specs=(P(GX_GY_GZ), P(None, GX_GY_GZ), P(GX_GY_GZ)),
        check_vma=False,
    )
```

profile of v0, /device:TPU:1, one launch (start us, length us, event | category | flops | bytes accessed | tf_op | source)
XLA Modules:
  0.0 1083.7 jit_solution(7078606515865511434)
XLA Ops:
  16.3 10.1 psum.168
  27.2 16.9 %psum.169 = f32[]{:T(128)} all-reduce(f32[]{:T(128)} %psum.168), channel_id=1, replica_groups=mesh['gx'=4,'gy'=8,'gz_0'=4,'gz_1'=2] {'gy'}, use_global_device_ids=true, to_apply=%region_2.3 | all-reduce | flops 1 | bytes 8 | tf_op jit(solution)/shard_map/psum | solution.py:21
  44.8 9.1 psum.170
  55.7 11.5 %psum.171 = f32[]{:T(128)} all-reduce(f32[]{:T(128)} %psum.170), channel_id=1, replica_groups=mesh['gx'=4,'gy'=8,'gz_0'=4,'gz_1'=2] {'gz_1'}, use_global_device_ids=true, to_apply=%region_4.5 | all-reduce | flops 1 | bytes 8 | tf_op jit(solution)/shard_map/psum | solution.py:21
  77.1 16.3 %broadcast_multiply_fusion.1 = f32[52,28,8192]{2,0,1:T(8,128)} fusion(f32[28,8192]{1,0:T(8,128)S(1)} %get-tuple-element.68, f32[52,8192]{1,0:T(8,128)S(1)} %broadcast_multiply_fusion.3), kind=kLoop, calls=%fused_computation.6 | loop fusion | flops 11927552 | bytes 50331648 | tf_op jit(solution)/shard_map/mul | solution.py:185
  93.5 36.0 %copy.88 = f32[52,28,8192]{2,1,0:T(8,128)} copy(f32[52,28,8192]{2,0,1:T(8,128)} %broadcast_multiply_fusion.1) | data formatting | bytes 95420416 | tf_op jit(solution)/shard_map/mul | solution.py:185
  129.4 42.0 %mul.899 = f32[1456,8192]{1,0:T(8,128)} reshape(f32[52,28,8192]{2,1,0:T(8,128)} %copy.88) | data formatting | bytes 95420416 | tf_op jit(solution)/shard_map/mul | solution.py:185
  171.5 44.6 %fusion.415 = f32[1456,28]{0,1:T(8,128)S(1)} fusion(f32[1456,8192]{1,0:T(8,128)} %mul.899, f32[8192]{0:T(1024)S(1)} %bitcast.557, s32[8192]{0:T(1024)S(1)} %bitcast.532, f32[8192]{0:T(1024)S(1)} %bitcast.552, s32[8192]{0:T(1024)S(1)} %bitcast.526, f32[8192]{0:T(1024)S(1)} %bitcast.547, s32[8192]{0:T(1024)S(1)} %bitcast.520, f32[8192]{0:T(1024)S(1)} %bitcast.542, ...), kind=kOutput, calls=%fused_computation.502 | convolution fusion | flops 4010868736 | bytes 48200960 | tf_op jit(solution)/shard_map/dot_general | solution.py:186
  243.0 6.2 all-to-all-start
  249.8 4.5 all-to-all-done
  259.0 4.3 all-to-all-start.2
  265.7 5.4 all-to-all-done.2
  291.0 6.7 all-to-all-start.3
  300.1 5.2 all-to-all-done.3
  305.3 4.2 all-to-all-start.4
  327.6 6.4 all-to-all-start.5
  366.4 5.2 all-to-all-done.7
  389.1 11.3 %all_to_all.360 = f32[8,1,3456]{2,1,0:T(1,128)S(1)} all-to-all(f32[8,1,3456]{2,1,0:T(1,128)S(1)} %reshape.1125), channel_id=1, replica_groups=mesh['gx'=4,'gy'=8,'gz_0'=4,'gz_1'=2] {'gz_0','gz_1'}, dimensions={0} | all-to-all | bytes 221184 | tf_op jit(solution)/shard_map/all_to_all | solution.py:160
  405.2 6.3 collective-permute-done.6
  422.8 42.4 %multiply_reduce_fusion.4 = f32[52,8192]{1,0:T(8,128)S(1)} fusion(f32[28,8192]{1,0:T(8,128)S(1)} %copy-done.6, f32[52,28,28]{0,2,1:T(8,128)S(1)} %pad_maximum_fusion.4, f32[8192]{0:T(1024)S(1)} %bitcast.559, s32[8192]{0:T(1024)S(1)} %bitcast.533, f32[8192]{0:T(1024)S(1)} %bitcast.554, s32[8192]{0:T(1024)S(1)} %bitcast.527, f32[8192]{0:T(1024)S(1)} %bitcast.549, ...), kind=kOutput, calls=%fused_computation.4 | convolution fusion | flops 4034297856 | bytes 3112192 | tf_op jit(solution)/shard_map/dot_general | solution.py:192
  467.2 9.7 all-reduce.8
  476.9 14.3 %all-reduce.6 = (f32[]{:T(128)}, f32[]{:T(128)}, f32[]{:T(128)}) all-reduce(f32[]{:T(128)} %get-tuple-element.20, f32[]{:T(128)} %get-tuple-element.21, f32[]{:T(128)} %get-tuple-element.22), channel_id=1, replica_groups=mesh['gx'=4,'gy'=8,'gz_0'=4,'gz_1'=2] {'gy'}, use_global_device_ids=true, to_apply=%region_21.22 | all-reduce | flops 3 | bytes 24 | tf_op jit(solution)/shard_map/psum | solution.py:21
  491.2 10.0 all-reduce.7
  501.2 7.8 all-reduce.9
  511.5 6.7 psum.184
  518.2 11.3 %psum.185 = f32[]{:T(128)} all-reduce(f32[]{:T(128)} %psum.184), channel_id=1, replica_groups=mesh['gx'=4,'gy'=8,'gz_0'=4,'gz_1'=2] {'gy'}, use_global_device_ids=true, to_apply=%region_26.27 | all-reduce | flops 1 | bytes 8 | tf_op jit(solution)/shard_map/psum | solution.py:21
  529.5 8.3 psum.186
  537.8 10.2 psum.187
  551.1 16.4 %broadcast_multiply_fusion = f32[52,28,8192]{2,0,1:T(8,128)} fusion(f32[52,8192]{1,0:T(8,128)S(1)} %broadcast_multiply_fusion.2, f32[28,8192]{1,0:T(8,128)S(1)} %copy-done.6), kind=kLoop, calls=%fused_computation.5 | loop fusion | flops 11927552 | bytes 50331648 | tf_op jit(solution)/shard_map/mul | solution.py:185
  567.5 36.0 %copy.129 = f32[52,28,8192]{2,1,0:T(8,128)} copy(f32[52,28,8192]{2,0,1:T(8,128)} %broadcast_multiply_fusion) | data formatting | bytes 95420416 | tf_op jit(solution)/shard_map/mul | solution.py:185
  603.6 42.1 %mul.928 = f32[1456,8192]{1,0:T(8,128)} reshape(f32[52,28,8192]{2,1,0:T(8,128)} %copy.129) | data formatting | bytes 95420416 | tf_op jit(solution)/shard_map/mul | solution.py:185
  645.7 44.6 %fusion.414 = f32[1456,28]{0,1:T(8,128)S(1)} fusion(f32[1456,8192]{1,0:T(8,128)} %mul.928, f32[8192]{0:T(1024)S(1)} %bitcast.560, s32[8192]{0:T(1024)S(1)} %bitcast.534, f32[8192]{0:T(1024)S(1)} %bitcast.555, s32[8192]{0:T(1024)S(1)} %bitcast.528, f32[8192]{0:T(1024)S(1)} %bitcast.550, s32[8192]{0:T(1024)S(1)} %bitcast.522, f32[8192]{0:T(1024)S(1)} %bitcast.545, ...), kind=kOutput, calls=%fused_computation.501 | convolution fusion | flops 4010868736 | bytes 48200960 | tf_op jit(solution)/shard_map/dot_general | solution.py:186
  716.7 10.7 all_to_all.361
  737.5 5.3 all-to-all-done.12
  762.8 6.7 all-to-all-start.13
  771.9 5.2 all-to-all-done.13
  777.1 4.4 all-to-all-start.14
  799.6 6.1 all-to-all-start.15
  838.2 5.2 all-to-all-done.17
  860.9 11.3 %all_to_all.362 = f32[8,1,3456]{2,1,0:T(1,128)S(1)} all-to-all(f32[8,1,3456]{2,1,0:T(1,128)S(1)} %reshape.1145), channel_id=1, replica_groups=mesh['gx'=4,'gy'=8,'gz_0'=4,'gz_1'=2] {'gz_0','gz_1'}, dimensions={0} | all-to-all | bytes 221184 | tf_op jit(solution)/shard_map/all_to_all | solution.py:160
  877.0 6.3 collective-permute-done.18
  894.6 42.6 %multiply_reduce_fusion.3 = f32[52,8192]{1,0:T(8,128)S(1)} fusion(f32[28,8192]{1,0:T(8,128)S(1)} %copy-done.7, f32[52,28,28]{0,2,1:T(8,128)S(1)} %pad_maximum_fusion.5, f32[8192]{0:T(1024)S(1)} %bitcast.561, s32[8192]{0:T(1024)S(1)} %bitcast.535, f32[8192]{0:T(1024)S(1)} %bitcast.556, s32[8192]{0:T(1024)S(1)} %bitcast.529, f32[8192]{0:T(1024)S(1)} %bitcast.551, ...), kind=kOutput, calls=%fused_computation.3 | convolution fusion | flops 4034297856 | bytes 3112192 | tf_op jit(solution)/shard_map/dot_general | solution.py:192
  939.1 9.2 psum.188
  948.4 14.2 %psum.189 = f32[]{:T(128)} all-reduce(f32[]{:T(128)} %psum.188), channel_id=1, replica_groups=mesh['gx'=4,'gy'=8,'gz_0'=4,'gz_1'=2] {'gy'}, use_global_device_ids=true, to_apply=%region_33.34 | all-reduce | flops 1 | bytes 8 | tf_op jit(solution)/shard_map/psum | solution.py:21
  962.6 9.9 psum.190
  972.5 7.7 psum.191
  981.6 50.4 %multiply_reduce_fusion.2 = (f32[52,8192]{1,0:T(8,128)S(1)}, f32[52,8192]{1,0:T(8,128)S(1)}) fusion(f32[28,8192]{1,0:T(8,128)S(1)} %copy-done.7, f32[28,8192]{1,0:T(8,128)} %get-tuple-element.67, f32[8192]{0:T(1024)} %bitcast.558, s32[8192]{0:T(1024)} %bitcast.531, f32[8192]{0:T(1024)} %bitcast.553, s32[8192]{0:T(1024)} %bitcast.525, f32[8192]{0:T(1024)} %bitcast.548, ...), kind=kOutput, calls=%fused_computation.2 | convolution fusion | flops 4057849344 | bytes 5896712 | tf_op jit(solution)/shard_map/dot_general | solution.py:192
  1038.1 42.2 %multiply_reduce_fusion = f32[52,8192]{1,0:T(8,128)S(1)} fusion(f32[28,8192]{1,0:T(8,128)S(1)} %copy-done.7, f32[8192]{0:T(1024)S(1)} %bitcast.652, f32[8192]{0:T(1024)S(1)} %bitcast.651, f32[8192]{0:T(1024)S(1)} %bitcast.650, f32[8192]{0:T(1024)S(1)} %bitcast.649, f32[8192]{0:T(1024)S(1)} %bitcast.653, s32[8192]{0:T(1024)S(1)} %bitcast.536, ...), kind=kOutput, calls=%fused_computation | convolution fusion | flops 4034420224 | bytes 3275272 | tf_op jit(solution)/shard_map/dot_general | solution.py:192
  (583 shorter events, 324.8 us)
Async XLA Ops:
  7.6 163.8 %copy-start.42 = (s32[1,8192]{1,0:T(1,128)}, s32[1,8192]{1,0:T(1,128)S(1)}, u32[]{:S(2)}) copy-start(s32[1,8192]{1,0:T(1,128)S(1)} %get-tuple-element.84) | copy-start | bytes 98308
  55.7 115.7 %copy-start.83 = (f32[1,8192]{1,0:T(1,128)}, f32[1,8192]{1,0:T(1,128)S(1)}, u32[]{:S(2)}) copy-start(f32[1,8192]{1,0:T(1,128)S(1)} %get-tuple-element.111) | copy-start | bytes 98308
  68.0 103.5 %copy-start.67 = (f32[1,8192]{1,0:T(1,128)}, f32[1,8192]{1,0:T(1,128)S(1)}, u32[]{:S(2)}) copy-start(f32[1,8192]{1,0:T(1,128)S(1)} %get-tuple-element.120) | copy-start | bytes 98308
  70.1 101.4 %copy-start.71 = (f32[1,8192]{1,0:T(1,128)}, f32[1,8192]{1,0:T(1,128)S(1)}, u32[]{:S(2)}) copy-start(f32[1,8192]{1,0:T(1,128)S(1)} %get-tuple-element.123) | copy-start | bytes 98308
  71.9 99.5 %copy-start.75 = (f32[1,8192]{1,0:T(1,128)}, f32[1,8192]{1,0:T(1,128)S(1)}, u32[]{:S(2)}) copy-start(f32[1,8192]{1,0:T(1,128)S(1)} %get-tuple-element.126) | copy-start | bytes 98308
  72.7 98.8 %copy-start.79 = (f32[1,8192]{1,0:T(1,128)}, f32[1,8192]{1,0:T(1,128)S(1)}, u32[]{:S(2)}) copy-start(f32[1,8192]{1,0:T(1,128)S(1)} %get-tuple-element.129) | copy-start | bytes 98308
  216.3 2.8 collective-permute-start.1
  216.5 4.0 collective-permute-start
  225.0 5.7 collective-permute-start.3
  225.5 4.0 collective-permute-start.2
  233.0 3.4 collective-permute-start.4
  234.9 3.6 collective-permute-start.5
  243.0 11.3 %all-to-all-start = ((f32[8,1,3456]{2,1,0:T(1,128)}), f32[8,1,3456]{2,1,0:T(1,128)S(1)}, u32[]{:S(2)}, u32[]{:S(2)}) async-start(f32[8,1,3456]{2,1,0:T(1,128)} %reshape.1107), calls=%async_computation | async-start | bytes 221184 | tf_op jit(solution)/shard_map/all_to_all | solution.py:131
  259.0 12.1 %all-to-all-start.2 = ((f32[8,1,3456]{2,1,0:T(1,128)}), f32[8,1,3456]{2,1,0:T(1,128)S(1)}, u32[]{:S(2)}, u32[]{:S(2)}) async-start(f32[8,1,3456]{2,1,0:T(1,128)} %reshape.1111), calls=%async_computation.2 | async-start | bytes 221184 | tf_op jit(solution)/shard_map/all_to_all | solution.py:136
  271.1 12.0 %all-to-all-start.1 = ((f32[8,1,3456]{2,1,0:T(1,128)}), f32[8,1,3456]{2,1,0:T(1,128)}, u32[]{:S(2)}, u32[]{:S(2)}) async-start(f32[8,1,3456]{2,1,0:T(1,128)} %reshape.1109), calls=%async_computation.1 | async-start | bytes 221184 | tf_op jit(solution)/shard_map/all_to_all | solution.py:135
  291.0 14.3 %all-to-all-start.3 = ((f32[32,1,864]{2,1,0:T(1,128)}), f32[32,1,864]{2,1,0:T(1,128)S(1)}, u32[]{:S(2)}, u32[]{:S(2)}) async-start(f32[32,1,864]{2,1,0:T(1,128)} %reshape.1113), calls=%async_computation.3 | async-start | bytes 229376 | tf_op jit(solution)/shard_map/all_to_all | solution.py:140
  305.3 11.7 %all-to-all-start.4 = ((f32[32,1,864]{2,1,0:T(1,128)}), f32[32,1,864]{2,1,0:T(1,128)S(1)}, u32[]{:S(2)}, u32[]{:S(2)}) async-start(f32[32,1,864]{2,1,0:T(1,128)} %reshape.1115), calls=%async_computation.4 | async-start | bytes 229376 | tf_op jit(solution)/shard_map/all_to_all | solution.py:141
  327.6 13.7 %all-to-all-start.5 = ((f32[32,1,864]{2,1,0:T(1,128)}), f32[32,1,864]{2,1,0:T(1,128)S(1)}, u32[]{:S(2)}, u32[]{:S(2)}) async-start(f32[32,1,864]{2,1,0:T(1,128)} %reshape.1117), calls=%async_computation.5 | async-start | bytes 229376 | tf_op jit(solution)/shard_map/all_to_all | solution.py:151
  341.3 11.5 %all-to-all-start.6 = ((f32[32,1,864]{2,1,0:T(1,128)}), f32[32,1,864]{2,1,0:T(1,128)S(1)}, u32[]{:S(2)}, u32[]{:S(2)}) async-start(f32[32,1,864]{2,1,0:T(1,128)} %reshape.1119), calls=%async_computation.6 | async-start | bytes 229376 | tf_op jit(solution)/shard_map/all_to_all | solution.py:152
  360.7 10.9 %all-to-all-start.7 = ((f32[8,1,3456]{2,1,0:T(1,128)}), f32[8,1,3456]{2,1,0:T(1,128)S(1)}, u32[]{:S(2)}, u32[]{:S(2)}) async-start(f32[8,1,3456]{2,1,0:T(1,128)} %reshape.1121), calls=%async_computation.7 | async-start | bytes 221184 | tf_op jit(solution)/shard_map/all_to_all | solution.py:156
  371.6 12.0 %all-to-all-start.8 = ((f32[8,1,3456]{2,1,0:T(1,128)}), f32[8,1,3456]{2,1,0:T(1,128)}, u32[]{:S(2)}, u32[]{:S(2)}) async-start(f32[8,1,3456]{2,1,0:T(1,128)} %reshape.1123), calls=%async_computation.8 | async-start | bytes 221184 | tf_op jit(solution)/shard_map/all_to_all | solution.py:157
  402.4 9.0 collective-permute-start.6
  403.8 7.7 collective-permute-start.7
  411.6 4.0 collective-permute-start.8
  411.9 3.6 collective-permute-start.9
  415.7 4.1 collective-permute-start.10
  418.8 3.6 collective-permute-start.11
  467.2 80.8 %copy-start.87 = (f32[8192]{0:T(1024)}, f32[8192]{0:T(1024)S(1)}, u32[]{:S(2)}) copy-start(f32[8192]{0:T(1024)S(1)} %get-tuple-element.38) | copy-start | bytes 98308
  690.6 3.1 collective-permute-start.13
  692.4 3.9 collective-permute-start.12
  699.3 4.5 collective-permute-start.14
  702.6 3.3 collective-permute-start.15
  708.3 3.8 collective-permute-start.16
  710.8 3.6 collective-permute-start.17
  731.6 11.3 %all-to-all-start.12 = ((f32[8,1,3456]{2,1,0:T(1,128)}), f32[8,1,3456]{2,1,0:T(1,128)S(1)}, u32[]{:S(2)}, u32[]{:S(2)}) async-start(f32[8,1,3456]{2,1,0:T(1,128)} %reshape.1131), calls=%async_computation.12 | async-start | bytes 221184 | tf_op jit(solution)/shard_map/all_to_all | solution.py:136
  742.9 12.0 %all-to-all-start.11 = ((f32[8,1,3456]{2,1,0:T(1,128)}), f32[8,1,3456]{2,1,0:T(1,128)}, u32[]{:S(2)}, u32[]{:S(2)}) async-start(f32[8,1,3456]{2,1,0:T(1,128)} %reshape.1129), calls=%async_computation.11 | async-start | bytes 221184 | tf_op jit(solution)/shard_map/all_to_all | solution.py:135
  762.8 14.3 %all-to-all-start.13 = ((f32[32,1,864]{2,1,0:T(1,128)}), f32[32,1,864]{2,1,0:T(1,128)S(1)}, u32[]{:S(2)}, u32[]{:S(2)}) async-start(f32[32,1,864]{2,1,0:T(1,128)} %reshape.1133), calls=%async_computation.13 | async-start | bytes 229376 | tf_op jit(solution)/shard_map/all_to_all | solution.py:140
  777.1 11.9 %all-to-all-start.14 = ((f32[32,1,864]{2,1,0:T(1,128)}), f32[32,1,864]{2,1,0:T(1,128)S(1)}, u32[]{:S(2)}, u32[]{:S(2)}) async-start(f32[32,1,864]{2,1,0:T(1,128)} %reshape.1135), calls=%async_computation.14 | async-start | bytes 229376 | tf_op jit(solution)/shard_map/all_to_all | solution.py:141
  799.6 13.5 %all-to-all-start.15 = ((f32[32,1,864]{2,1,0:T(1,128)}), f32[32,1,864]{2,1,0:T(1,128)S(1)}, u32[]{:S(2)}, u32[]{:S(2)}) async-start(f32[32,1,864]{2,1,0:T(1,128)} %reshape.1137), calls=%async_computation.15 | async-start | bytes 229376 | tf_op jit(solution)/shard_map/all_to_all | solution.py:151
  813.1 11.5 %all-to-all-start.16 = ((f32[32,1,864]{2,1,0:T(1,128)}), f32[32,1,864]{2,1,0:T(1,128)S(1)}, u32[]{:S(2)}, u32[]{:S(2)}) async-start(f32[32,1,864]{2,1,0:T(1,128)} %reshape.1139), calls=%async_computation.16 | async-start | bytes 229376 | tf_op jit(solution)/shard_map/all_to_all | solution.py:152
  832.5 10.9 %all-to-all-start.17 = ((f32[8,1,3456]{2,1,0:T(1,128)}), f32[8,1,3456]{2,1,0:T(1,128)S(1)}, u32[]{:S(2)}, u32[]{:S(2)}) async-start(f32[8,1,3456]{2,1,0:T(1,128)} %reshape.1141), calls=%async_computation.17 | async-start | bytes 221184 | tf_op jit(solution)/shard_map/all_to_all | solution.py:156
  843.4 12.0 %all-to-all-start.18 = ((f32[8,1,3456]{2,1,0:T(1,128)}), f32[8,1,3456]{2,1,0:T(1,128)}, u32[]{:S(2)}, u32[]{:S(2)}) async-start(f32[8,1,3456]{2,1,0:T(1,128)} %reshape.1143), calls=%async_computation.18 | async-start | bytes 221184 | tf_op jit(solution)/shard_map/all_to_all | solution.py:157
  874.2 9.0 collective-permute-start.18
  875.6 7.7 collective-permute-start.19
  883.4 4.0 collective-permute-start.20
  883.7 3.6 collective-permute-start.21
  887.5 4.0 collective-permute-start.22
  890.5 3.6 collective-permute-start.23
  (121 other events, 2723.6 us)
where the time goes:
time: 1100 us; the launch traced here: 1080 us
  matrix products  333 us (30%)
  local copies, waits for them, and re-layouts  240 us (22%)
  blocking collectives  200 us (18%)
  starting transfers between devices  111 us (10%)
  waiting for transfers between devices  100 us (9%)
  other arithmetic  89.5 us (8%)
    dot_general x4, matrix products, third_contract(): inner = jnp.dot(flat_rows, third_mask, precision=lax.Precision.HIGHEST)  178 us
    psum x16, blocking collectives, by_axis(): array = lax.psum(array, axis)  167 us
    mul x4, local copies, waits for them, and re-layouts, spread_local(): first_mask[:, None, :] * second_mask[None, :, :]  156 us
    dot_general x2, matrix products, spread_local(): grid = jnp.dot(paired, third_mask.T, precision=lax.Precision.HIGHEST)  89.3 us
    unnamed x32, matrix products  42.4 us
    mul x2, other arithmetic, spread_local(): first_mask[:, None, :] * second_mask[None, :, :]  32.8 us
    unnamed x296, local copies, waits for them, and re-layouts  28.6 us
    ppermute x12, waiting for transfers between devices, with_halo(): lax.ppermute(tail, axis, [(i, (i + 1) % count) for i in range(count)])  25 us
  transfers between devices with their start and end apart: 41, of which 35 were waited for; matrix products, arithmetic and copies ran while one was open for 6% of the time, Pallas kernels for 0%

commit v1 on v0

v1 whole, which is shorter than its diff:
```python
import functools
import math

import jax
import jax.numpy as jnp
import numpy as np
from jax import lax
from jax.experimental import pallas as pl
from jax.experimental.pallas import tpu as pltpu
from jax.sharding import PartitionSpec as P

M = 192
SMEAR = 0.75
GX, PAX, QAX = "gx", "gy", "gz"
P_DIM, Q_DIM = 1, 2
AXES = ("gx", "gy", "gz")
ATOMS = 8192
CH = 512
NCH = ATOMS // CH
XR = 56
LN = 256
F32, BF16 = jnp.float32, jnp.bfloat16
MESH = pl.DeviceIdType.MESH


def cas(rows, columns):
    angle = 2.0 * np.pi * ((rows[:, None] * columns[None, :]) % M) / M
    return np.cos(angle) + np.sin(angle)


def halves(array):
    array = np.asarray(array, np.float32)
    high = array.astype(jnp.bfloat16)
    low = (array - high.astype(np.float32)).astype(jnp.bfloat16)
    return np.stack([high, low])


def tables():
    freq = np.arange(M)
    cell_x = (48 * np.arange(4)[:, None] + np.arange(XR)[None, :] - 2).reshape(-1) % M
    real_x = np.tile(np.arange(XR) < 52, 4)
    h_x = cas(freq, cell_x) * real_x[None, :]
    cell_p = (24 * np.arange(8)[:, None] + np.arange(32)[None, :] - 2).reshape(-1) % M
    real_p = np.tile(np.arange(32) < 28, 8)
    row_p = np.arange(M)
    freq_p = (row_p % 32) * 6 + row_p // 32
    h_p = np.zeros((256, 256))
    h_p[:M] = cas(freq_p, cell_p) * real_p[None, :]
    src = np.arange(256) // 8
    part = np.arange(256) % 8
    cell_q = (24 * (src % 8) + 7 * (src // 8) + part - 2) % M
    h_q = cas(freq, cell_q) * (part < 7)[None, :]
    lanes = np.zeros((8, 256), np.float32)
    lanes[0, :144] = np.arange(144) // 24
    lanes[1, :144] = np.arange(144) % 24
    return halves(h_x), halves(h_x.T), halves(h_p), halves(h_q), halves(h_q.T), lanes


def split(value):
    high = value.astype(BF16)
    return high, (value - high.astype(F32)).astype(BF16)


def dot(left, right, dims=((1,), (0,))):
    return lax.dot_general(left, right, (dims, ((), ())), preferred_element_type=F32)


def dot3(table, value, dims=((1,), (0,))):
    high, low = split(value)
    return dot(table[0], high, dims) + (dot(table[0], low, dims) + dot(table[1], high, dims))


def signed(number):
    return jnp.where(2.0 * number >= M, number - M, number)


def peers_x(ix, iq):
    return [(step, {GX: lax.rem(ix + step, 4)}, lax.rem(ix + step, 4)) for step in (2, 1, 3)]


def peers_p(ip):
    return [(step, {PAX: lax.rem(ip + step, 8)}, lax.rem(ip + step, 8)) for step in (4, 3, 5, 2, 6, 1, 7)]


def peers_q(iq):
    return [(step, {QAX: lax.rem(iq + step, 8)}, lax.rem(iq + step, 8)) for step in (4, 3, 5, 2, 6, 1, 7)]


def peers_xq(ix, iq):
    steps = sorted(
        [(a, b) for a in range(4) for b in range(8) if a or b],
        key=lambda t: -(min(t[0], 4 - t[0]) + min(t[1], 8 - t[1])),
    )
    found = []
    for a, b in steps:
        g, h = lax.rem(ix + a, 4), lax.rem(iq + b, 8)
        found.append((a * 8 + b, {GX: g, QAX: h}, g * 8 + h))
    return found


def send_all(peers, src_of, dst, send, recv, base):
    copies = []
    for step, where, number in peers:
        copy = pltpu.make_async_remote_copy(
            src_ref=src_of(number),
            dst_ref=dst,
            send_sem=send.at[base + step],
            recv_sem=recv.at[base + step],
            device_id=where,
            device_id_type=MESH,
        )
        copy.start()
        copies.append(copy)
    return copies


def wait_all(copies):
    for copy in copies:
        copy.wait_recv()
    for copy in copies:
        copy.wait_send()


def rows8(start):
    return pl.ds(pl.multiple_of(start, 8), 8)


def comb_store(ref, row, value):
    for h in range(2):
        ref[h, pl.ds(row, 32, stride=8), :] = value[:, 128 * h : 128 * h + 128]


def lane_pick(pieces, width, length=LN):
    lane = lax.broadcasted_iota(jnp.int32, pieces[0][0].shape, 1)
    result = jnp.zeros(pieces[0][0].shape, F32)
    for number, (array, shift) in enumerate(pieces):
        shift = shift % length
        moved = array if shift == 0 else pltpu.roll(array, shift, 1)
        inside = (lane >= number * width) & (lane < (number + 1) * width)
        result = jnp.where(inside, moved, result)
    return result


def kernel(
    chi_ref, types_ref, offs_ref, base_ref, hard_ref,
    hx_ref, hxt_ref, hp_ref, hq_ref, hqt_ref, lanes_ref,
    charges_ref, forces_ref,
    w_ref, s_ref, mx_ref, mp_ref, mq_ref, a_ref, b_ref, acc_ref,
    ones_ref, sp_ref, sd_ref, r1_ref, k1_ref, r2_ref, x2_ref, m_ref, r3_ref, green_ref,
    z3_ref, r3b_ref, k3b_ref, m2b_ref, r2b_ref, v1_ref, r1b_ref, phi0_ref, phi_ref,
    image_ref, p0_ref, d1_ref, t_ref, arx_ref, arp_ref, arq_ref, ars_ref,
    send, recv,
):
    ix, ip, iq = lax.axis_index(GX), lax.axis_index(PAX), lax.axis_index(QAX)
    mine = ix * 8 + iq
    to_x, to_p, to_q, to_xq = peers_x(ix, iq), peers_p(ip), peers_q(iq), peers_xq(ix, iq)
    barrier = pltpu.get_barrier_semaphore()
    for _, where, _ in to_xq + to_p:
        pl.semaphore_signal(barrier, inc=1, device_id=where, device_id_type=MESH)

    hardness = jnp.where(
        types_ref[...] == 0, hard_ref[0], jnp.where(types_ref[...] == 1, hard_ref[1], hard_ref[2])
    )
    for d in range(3):
        t = offs_ref[d]
        spline = [t, 1.0 - t]
        for order in (3, 4, 5):
            grown = []
            for k in range(order):
                term = None
                if k < order - 1:
                    term = (t + k) * spline[k]
                if k >= 1:
                    other = (order - k - t) * spline[k - 1]
                    term = other if term is None else term + other
                grown.append(term * (1.0 / (order - 1)))
            if order == 5:
                s_ref[d, 0] = -spline[3]
                s_ref[d, 1] = spline[3] - spline[2]
                s_ref[d, 2] = spline[2] - spline[1]
                s_ref[d, 3] = spline[1] - spline[0]
                s_ref[d, 4] = spline[0]
            spline = grown
        for j in range(5):
            w_ref[d, j] = spline[4 - j]

    row = lax.broadcasted_iota(jnp.int32, (M, LN), 0).astype(F32)
    f_q = signed(row)
    f_p = signed(lanes_ref[0:1, :] + (6 * mine).astype(F32))
    f_x = signed(lanes_ref[1:2, :] + (24 * ip).astype(F32))
    factor = 2.0 * math.pi / M
    wave = (factor * factor) * (f_q * f_q + (f_p * f_p + f_x * f_x))
    safe = jnp.where(wave > 0, wave, 1.0)
    green_ref[...] = jnp.where(
        wave > 0, (4.0 * math.pi / (M * M * M)) * jnp.exp((-0.5 * SMEAR * SMEAR) * wave) / safe, 0.0
    )

    zero8 = jnp.zeros((8, LN), F32)
    for g in range(4):
        r1b_ref[g, XR : XR + 8, :] = zero8
        acc_ref[256 * g + 224 : 256 * g + 256, :] = jnp.zeros((32, 256), F32)
    x2_ref[168:256, :] = jnp.zeros((88, LN), F32)
    comb_store(m_ref, 7, jnp.zeros((32, LN), F32))
    k3b_ref[192:256, :] = jnp.zeros((64, LN), F32)

    def mask(table, d, c, count):
        base = base_ref[d, pl.ds(c, 1), :]
        place = lax.broadcasted_iota(jnp.int32, (count, CH), 0) - base
        result = jnp.zeros((count, CH), F32)
        for j in range(5):
            result = jnp.where(place == j, table[d, j, pl.ds(c, 1), :], result)
        return result

    def spread(values_ref, shift, lo, hi, first):
        def step(c, carry):
            if first:
                m_x, m_p, m_q = mask(w_ref, 0, c, 64), mask(w_ref, P_DIM, c, 32), mask(w_ref, Q_DIM, c, 32)
                mx_ref[c], mp_ref[c], mq_ref[c] = m_x, m_p, m_q
                for q in range(28):
                    high, low = split(m_p * m_q[q : q + 1, :])
                    a_ref[c, 32 * q : 32 * q + 32, :] = high
                    a_ref[c, 896 + 32 * q : 896 + 32 * q + 32, :] = low
                b_ref[128:192, :], b_ref[192:256, :] = split(m_x)
            else:
                m_x = mx_ref[c]
            b_ref[0:64, :], b_ref[64:128, :] = split(m_x * (values_ref[pl.ds(c, 1), :] - shift))
            width = 256 if first else 128
            part = dot(a_ref[c], b_ref[0:width, :], ((1,), (1,)))
            for g in range(4):
                acc_ref[256 * g : 256 * g + 224, 0:width] += (
                    part[224 * g : 224 * g + 224] + part[896 + 224 * g : 896 + 224 * g + 224]
                )
            return carry

        lax.fori_loop(lo, hi, step, 0)

    def clear(width):
        for g in range(4):
            acc_ref[256 * g : 256 * g + 224, 0:width] = jnp.zeros((224, width), F32)

    lane = lax.broadcasted_iota(jnp.int32, (8, 128), 1)

    def pack(sums):
        tile = jnp.zeros((8, 128), F32)
        for k, value in enumerate(sums):
            tile = jnp.where(lane == k, value, tile)
        return tile

    def total(array):
        return jnp.sum(jnp.sum(array, axis=0, keepdims=True), axis=1, keepdims=True)

    def ar_start(phase, tile):
        peers, slots, me, base = (
            (to_x, arx_ref, ix, 100), (to_p, arp_ref, ip, 104), (to_q, arq_ref, iq, 112)
        )[phase]
        slots[me] = tile
        ars_ref[phase] = tile
        return send_all(peers, lambda number: ars_ref.at[phase], slots.at[me], send, recv, base)

    def ar_done(phase, copies):
        wait_all(copies)
        return jnp.sum((arx_ref, arp_ref, arq_ref)[phase][...], axis=0)

    def solve():
        r1_ref[ix] = sd_ref[ix, 0:XR, :]
        copies = send_all(to_x, lambda g: sd_ref.at[g, 0:XR], r1_ref.at[ix], send, recv, 0)
        wait_all(copies)
        k1 = dot3(hx_ref, r1_ref[...].reshape(4 * XR, LN))
        k1_ref[...] = k1.reshape(8, 24, LN)
        r2_ref[ip] = k1_ref[ip]
        copies = send_all(to_p, lambda s: k1_ref.at[s], r2_ref.at[ip], send, recv, 4)
        wait_all(copies)
        for y in range(7):
            x2_ref[24 * y : 24 * y + 24, :] = lane_pick(
                [(r2_ref[s], 32 * (s - y)) for s in range(8)], 32
            )
        k2 = dot3((hp_ref[0, 0:M, :], hp_ref[1, 0:M, :]), x2_ref[...], ((1,), (1,)))
        for y in range(7):
            comb_store(
                m_ref,
                y,
                lane_pick([(k2[32 * k : 32 * k + 32, :], 24 * (k - y)) for k in range(6)], 24),
            )
        r3_ref[:, rows8(8 * mine), :] = m_ref[:, rows8(8 * mine), :]
        copies = send_all(
            to_xq, lambda n: m_ref.at[:, rows8(8 * n)], r3_ref.at[:, rows8(8 * mine)], send, recv, 12
        )
        wait_all(copies)
        k3 = dot3(hq_ref, jnp.concatenate([r3_ref[0], r3_ref[1]], axis=1)) * green_ref[...]
        z3 = dot3(hqt_ref, k3)
        z3_ref[0], z3_ref[1] = z3[:, 0:128], z3[:, 128:256]
        r3b_ref[:, rows8(8 * mine), :] = z3_ref[:, rows8(8 * mine), :]
        copies = send_all(
            to_xq, lambda n: z3_ref.at[:, rows8(8 * n)], r3b_ref.at[:, rows8(8 * mine)], send, recv, 44
        )
        wait_all(copies)
        loaded = [
            jnp.concatenate([r3b_ref[h, pl.ds(y, 32, stride=8), :] for h in range(2)], axis=1)
            for y in range(7)
        ]
        for k in range(6):
            k3b_ref[32 * k : 32 * k + 32, :] = lane_pick(
                [(loaded[y], 24 * (y - k)) for y in range(7)], 24
            )
        turned = jnp.transpose(k3b_ref[...])
        high, low = split(turned)
        v2 = dot(high, hp_ref[0]) + (dot(low, hp_ref[0]) + dot(high, hp_ref[1]))
        for s in range(8):
            m2b_ref[s] = lane_pick(
                [(v2[24 * y : 24 * y + 24, :], 32 * (y - s)) for y in range(7)], 32
            )
        r2b_ref[ip] = m2b_ref[ip]
        copies = send_all(to_p, lambda s: m2b_ref.at[s], r2b_ref.at[ip], send, recv, 76)
        wait_all(copies)
        v1_ref[...] = dot3(hxt_ref, r2b_ref[...].reshape(M, LN)).reshape(4, XR, LN)
        r1b_ref[ix, 0:XR, :] = v1_ref[ix]
        copies = send_all(to_x, lambda g: v1_ref.at[g], r1b_ref.at[ix, 0:XR], send, recv, 84)
        wait_all(copies)

    def load_field(get):
        for g in range(4):
            high, low = split(get(g))
            both = jnp.concatenate([high.astype(F32), low.astype(F32)], axis=0)
            turned = jnp.transpose(both)[0:224, :].astype(BF16)
            phi_ref[224 * g : 224 * g + 224, 0:128] = turned
            phi_ref[224 * g : 224 * g + 224, 128:256] = turned

    def x_contract(m_x, slot):
        high, low = split(m_x)
        b_ref[0:64, :], b_ref[64:128, :], b_ref[128:192, :], b_ref[192:256, :] = high, high, low, low
        t_ref[slot] = dot(phi_ref[...], b_ref[...])

    def fold(product):
        return (product[0:8] + product[8:16]) + (product[16:24] + product[24:32])

    def sample_image(values_ref):
        def step(c, carry):
            x_contract(mx_ref[c], 0)
            m_p = mp_ref[c]
            found = jnp.zeros((8, CH), F32)
            for q in range(28):
                found = found + fold(t_ref[0, 32 * q : 32 * q + 32, :] * m_p) * mq_ref[c, q : q + 1, :]
            image_ref[pl.ds(c, 1), :] = jnp.sum(found, axis=0, keepdims=True)
            return carry

        lax.fori_loop(0, NCH, step, 0)
        image_ref[...] = image_ref[...] + hardness * values_ref[...]

    def sample_forces():
        def step(c, carry):
            m_p, s_p = mp_ref[c], mask(s_ref, P_DIM, c, 32)
            b = mask(s_ref, Q_DIM, c, 32)
            x_contract(mx_ref[c], 0)
            x_contract(mask(s_ref, 0, c, 64), 1)
            along_x, along_p, along_q = (jnp.zeros((8, CH), F32) for _ in range(3))
            for q in range(28):
                block = t_ref[0, 32 * q : 32 * q + 32, :]
                m_q = mq_ref[c, q : q + 1, :]
                along_q = along_q + fold(block * m_p) * b[q : q + 1, :]
                along_p = along_p + fold(block * s_p) * m_q
                along_x = along_x + fold(t_ref[1, 32 * q : 32 * q + 32, :] * m_p) * m_q
            minus = -charges_ref[pl.ds(c, 1), :]
            forces_ref[0, pl.ds(c, 1), :] = minus * jnp.sum(along_x, axis=0, keepdims=True)
            forces_ref[P_DIM, pl.ds(c, 1), :] = minus * jnp.sum(along_p, axis=0, keepdims=True)
            forces_ref[Q_DIM, pl.ds(c, 1), :] = minus * jnp.sum(along_q, axis=0, keepdims=True)
            return carry

        lax.fori_loop(0, NCH, step, 0)

    atoms = float(ATOMS * 256)
    clear(256)
    chi = chi_ref[...]
    local_sum = total(chi)
    shift = local_sum * (1.0 / ATOMS)
    pl.semaphore_wait(barrier, len(to_xq) + len(to_p))
    copies = ar_start(0, pack([local_sum]))
    spread(chi_ref, shift, 0, 5, True)
    copies = ar_start(1, ar_done(0, copies))
    spread(chi_ref, shift, 5, 11, True)
    copies = ar_start(2, ar_done(1, copies))
    spread(chi_ref, shift, 11, NCH, True)
    mean = ar_done(2, copies)[0:1, 0:1] * (1.0 / atoms)
    for g in range(4):
        turned = jnp.transpose(acc_ref[256 * g : 256 * g + 256, :])
        ones = turned[128:192] + turned[192:256]
        ones_ref[g] = ones
        field = (mean - shift) * ones - (turned[0:64] + turned[64:128])
        sp_ref[g] = field
        sd_ref[g] = field
    p0 = mean - chi
    p0_ref[...] = p0
    solve()
    for g in range(4):
        phi0_ref[g] = r1b_ref[g]
    load_field(lambda g: r1b_ref[g])
    sample_image(p0_ref)

    image = image_ref[...]
    image_sum = total(image)
    shift2 = image_sum * (1.0 / ATOMS)
    sums = pack([total(p0 * p0), total(p0 * image), image_sum, total(image * image), total(p0)])
    clear(128)
    copies = ar_start(0, sums)
    spread(image_ref, shift2, 0, 5, False)
    copies = ar_start(1, ar_done(0, copies))
    spread(image_ref, shift2, 5, 11, False)
    copies = ar_start(2, ar_done(1, copies))
    spread(image_ref, shift2, 11, NCH, False)
    sums = ar_done(2, copies)
    norm0, curve0, image_total, image_square, p0_total = (sums[0:1, k : k + 1] for k in range(5))
    alpha0 = norm0 / curve0
    image_mean = image_total * (1.0 / atoms)
    norm1 = (
        norm0
        - 2.0 * alpha0 * (curve0 - image_mean * p0_total)
        + alpha0 * alpha0 * (image_square - image_mean * image_total)
    )
    beta = norm1 / norm0
    residual = p0 - alpha0 * (image - image_mean)
    d1_ref[...] = residual + beta * p0
    for g in range(4):
        turned = jnp.transpose(acc_ref[256 * g : 256 * g + 256, 0:128])
        sd_ref[g] = (
            (1.0 + beta) * sp_ref[g]
            + (alpha0 * (image_mean - shift2)) * ones_ref[g]
            - alpha0 * (turned[0:64] + turned[64:128])
        )
    solve()
    load_field(lambda g: r1b_ref[g])
    sample_image(d1_ref)
    d1 = d1_ref[...]
    sums = pack([total(residual * residual), total(d1 * image_ref[...])])
    copies = ar_start(0, sums)
    copies = ar_start(1, ar_done(0, copies))
    copies = ar_start(2, ar_done(1, copies))
    sums = ar_done(2, copies)
    alpha1 = sums[0:1, 0:1] / sums[0:1, 1:2]
    charges_ref[...] = alpha0 * p0_ref[...] + alpha1 * d1
    load_field(lambda g: alpha0 * phi0_ref[g] + alpha1 * r1b_ref[g])
    sample_forces()


def equilibrate(chi, types, offsets, stencil_base, hardness):
    tabs = tables()
    vmem = pl.BlockSpec(memory_space=pltpu.VMEM)
    smem = pl.BlockSpec(memory_space=pltpu.SMEM)

    def held(*shape, dtype=F32):
        return pltpu.VMEM(shape, dtype)

    return pl.pallas_call(
        kernel,
        out_shape=(
            jax.ShapeDtypeStruct((NCH, CH), F32),
            jax.ShapeDtypeStruct((3, NCH, CH), F32),
        ),
        in_specs=[vmem] * 4 + [smem] + [vmem] * 6,
        out_specs=(vmem, vmem),
        scratch_shapes=[
            held(3, 5, NCH, CH), held(3, 5, NCH, CH),
            held(NCH, 64, CH), held(NCH, 32, CH), held(NCH, 32, CH),
            held(NCH, 1792, CH, dtype=BF16), held(256, CH, dtype=BF16),
            held(1024, 256),
            held(4, 64, LN), held(4, 64, LN), held(4, 64, LN),
            held(4, XR, LN), held(8, 24, LN), held(8, 24, LN),
            held(256, LN), held(2, 256, 128), held(2, 256, 128), held(M, LN),
            held(2, 256, 128), held(2, 256, 128), held(256, LN),
            held(8, 24, LN), held(8, 24, LN), held(4, XR, LN),
            held(4, 64, LN), held(4, 64, LN), held(896, 256, dtype=BF16),
            held(NCH, CH), held(NCH, CH), held(NCH, CH),
            held(2, 896, CH),
            held(4, 8, 128), held(8, 8, 128), held(8, 8, 128), held(3, 8, 128),
            pltpu.SemaphoreType.DMA((120,)),
            pltpu.SemaphoreType.DMA((120,)),
        ],
        compiler_params=pltpu.CompilerParams(
            collective_id=0, has_side_effects=True, vmem_limit_bytes=60 * 1024 * 1024
        ),
        name="equilibrate",
    )(
        chi.reshape(NCH, CH), types.reshape(NCH, CH), offsets.reshape(3, NCH, CH),
        stencil_base.reshape(3, NCH, CH), hardness, *[jnp.asarray(t) for t in tabs],
    )


def element_net(first, second, final, descriptors, onehot):
    hidden = jnp.tanh(
        jnp.einsum("ehf,fa->eha", first, descriptors, precision=lax.Precision.HIGHEST)
    )
    hidden = jnp.tanh(jnp.einsum("ehg,ega->eha", second, hidden, precision=lax.Precision.HIGHEST))
    output = jnp.einsum("eh,eha->ea", final, hidden, precision=lax.Precision.HIGHEST)
    return jnp.sum(onehot * output, axis=0)


def per_device(
    descriptors, types, offsets, stencil_base, w_first, w_second, w_out, hardness,
    sr_first, sr_charge, sr_out,
):
    elements = w_first.shape[0]
    onehot = (types[None, :] == jnp.arange(elements, dtype=jnp.int32)[:, None]).astype(F32)
    chi = element_net(w_first, w_second, w_out, descriptors, onehot)
    charges, forces = equilibrate(chi, types, offsets, stencil_base, hardness)
    charges = charges.reshape(ATOMS)
    forces = forces.reshape(3, ATOMS)
    hidden = jnp.tanh(
        jnp.einsum("ehf,fa->eha", sr_first, descriptors, precision=lax.Precision.HIGHEST)
        + sr_charge[:, :, None] * charges[None, None, :]
    )
    short_energy = jnp.sum(
        onehot * jnp.einsum("eh,eha->ea", sr_out, hidden, precision=lax.Precision.HIGHEST), axis=0
    )
    return charges, forces, short_energy


def solution(mesh):
    rows, columns = P(AXES), P(None, AXES)
    return jax.shard_map(
        per_device,
        mesh=mesh,
        in_specs=(columns, rows, columns, columns) + (P(),) * 7,
        out_specs=(rows, columns, rows),
        check_vma=False,
    )
```

time: 1100 us -> 173 us (0.16); the launches traced: 1080 us -> 173 us
  matrix products: 333 us -> 13.4 us
  local copies, waits for them, and re-layouts: 240 us -> 5.71 us
  blocking collectives: 200 us -> 0 us
  Pallas kernels: 0 us -> 152 us
  starting transfers between devices: 111 us -> 0 us
  waiting for transfers between devices: 100 us -> 0 us
  other arithmetic: 89.5 us -> 0.88 us
    dot_general x14 -> x0, matrix products: 278 us -> none  [the longest x4 178 us: third_contract(): inner = jnp.dot(flat_rows, third_mask, precision=lax.Precision.HIGHEST)]
    psum x16 -> x0, blocking collectives: 167 us -> none  [by_axis(): array = lax.psum(array, axis)]
    mul x4 -> x0, local copies, waits for them, and re-layouts: 156 us -> none  [spread_local(): first_mask[:, None, :] * second_mask[None, :, :]]
    pallas_call x0 -> x1, Pallas kernels: none -> 152 us  [equilibrate(): pl.pallas_call(kernel, out_shape=(jax.ShapeDtypeStruct((NCH, CH), F32), j...]
    all_to_all x17 -> x0, starting transfers between devices: 79.7 us -> none  [the longest x2 13.4 us: spectral(): lax.all_to_all(real_part, GX_GZ, split_axis=1, concat_axis=0, tiled=True)]
    all_to_all x17 -> x0, waiting for transfers between devices: 62.9 us -> none  [the longest x2 10.7 us: spectral(): lax.all_to_all(imag_part, 'gy', split_axis=2, concat_axis=1, tiled=True)]
    unnamed x32 -> x0, matrix products: 42.4 us -> none
    ppermute x24 -> x0, waiting for transfers between devices: 37.1 us -> none  [the longest x12 25 us: with_halo(): lax.ppermute(tail, axis, [(i, (i + 1) % count) for i in range(count)])]
  transfers between devices with their start and end apart: 41 -> 0, of which waited for: 35 -> 0; matrix products, arithmetic and copies ran while one was open for 6% -> 0% of each run, Pallas kernels for 0% -> 0%
where the time goes in v1:
time: 173 us
  Pallas kernels  152 us (88%)
  matrix products  13.4 us (8%)
  local copies, waits for them, and re-layouts  5.71 us (3%)
    pallas_call x1, Pallas kernels, equilibrate(): pl.pallas_call(kernel, out_shape=(jax.ShapeDtypeStruct((NCH, CH), F32), j...  152 us
    unnamed x26, local copies, waits for them, and re-layouts  4.47 us
    dot_general x1, matrix products, element_net(): jnp.einsum('ehf,fa->eha', first, descriptors, precision=lax.Precision.HIG...  3.48 us

profile of v1, /device:TPU:1, one launch (start us, length us, event | category | flops | bytes accessed | tf_op | source)
XLA Modules:
  0.0 173.1 jit_solution(11548471150847071114)
XLA Ops:
  0.6 0.0 copy-start
  0.6 0.0 copy-start.6
  0.7 1.6 copy-done
  2.2 3.5 %convolution_tanh_fusion = f32[3,25,8192]{2,1,0:T(8,128)S(1)} fusion(f32[3,25,64]{2,1,0:T(8,128)} %param.21, f32[64,8192]{1,0:T(8,128)S(1)} %copy-done), kind=kOutput, calls=%fused_computation.2 | convolution fusion | flops 471859200 | bytes 4573952 | tf_op jit(solution)/shard_map/ehf,fa->eha/dot_general | solution.py:488
  5.7 0.0 copy-done.6
  5.7 0.0 copy-start.9
  5.7 3.0 %convolution_tanh_fusion.1 = f32[3,8192,25]{1,2,0:T(8,128)S(1)} fusion(f32[3,25,8192]{2,1,0:T(8,128)S(1)} %convolution_tanh_fusion, f32[3,25,25]{2,1,0:T(8,128)S(1)} %copy-done.6), kind=kOutput, calls=%fused_computation.3 | convolution fusion | flops 184320000 | bytes 4922700 | tf_op jit(solution)/shard_map/ehg,ega->eha/dot_general | solution.py:490
  8.8 0.0 copy-start.1
  8.8 0.0 copy-start.3
  8.8 0.0 copy-start.4
  8.8 0.0 copy-start.7
  8.8 0.0 copy-start.8
  8.8 0.0 copy-done.9
  8.8 2.0 %fusion.7 = f32[3,1,8192]{2,1,0:T(1,128)S(1)} fusion(f32[3,8192,25]{1,2,0:T(8,128)S(1)} %convolution_tanh_fusion.1, f32[3,25,1]{1,0,2:T(4,128)S(1)} %bitcast.42), kind=kOutput, calls=%fused_computation.15 | convolution fusion | flops 7372800 | bytes 2556204 | tf_op jit(solution)/shard_map/eh,eha->ea/dot_general | solution.py:491
  10.8 0.0 copy-done.1
  10.8 0.1 fusion.4
  11.0 0.6 reshape.27.chi_ref
  11.6 0.0 copy-done.3
  11.6 0.7 copy.36
  12.3 0.0 copy-done.4
  12.3 0.7 copy.37
  13.0 0.6 reshape.28.types_ref
  13.6 0.0 copy-start.10
  13.6 152.3 %equilibrate.1 = (f32[16,512]{1,0:T(8,128)}, f32[3,16,512]{2,1,0:T(8,128)}) custom-call(f32[16,512]{1,0:T(8,128)} %reshape.27.chi_ref, s32[16,512]{1,0:T(8,128)} %reshape.28.types_ref, f32[3,16,512]{2,1,0:T(8,128)} %bitcast.34, s32[3,16,512]{2,1,0:T(8,128)} %bitcast.33, f32[3]{0:T(128)} %hard_ref.1, bf16[2,192,224]{2,1,0:T(8,128)(2,1)} %constant.16.clone.hx_ref, ...), custom_call_target="tpu_custom_call" | custom-call | tf_op jit(solution)/shard_map/equilibrate/pallas_call | solution.py:451
  165.8 0.8 copy.26
  166.6 0.0 copy-start.2
  166.6 0.0 copy-done.7
  166.6 0.0 copy-done.8
  166.7 0.0 copy-start.5
  166.7 2.9 %fusion = f32[3,25,8192]{2,1,0:T(8,128)S(1)} fusion(f32[3,25,64]{2,1,0:T(8,128)S(1)} %copy-done.7, f32[64,8192]{1,0:T(8,128)S(1)} %copy-done, f32[8192]{0:T(1024)S(1)} %bitcast.35, f32[3,25]{1,0:T(4,128)S(1)} %copy-done.8), kind=kOutput, calls=%fused_computation.1 | convolution fusion | flops 473088000 | bytes 4607020 | tf_op jit(solution)/shard_map/ehf,fa->eha/dot_general | solution.py:506
  169.6 0.0 copy-done.10
  169.6 2.0 %fusion.5 = f32[3,1,8192]{2,1,0:T(1,128)S(1)} fusion(f32[3,25,8192]{2,1,0:T(8,128)S(1)} %fusion, f32[3,25,1]{1,0,2:T(4,128)S(1)} %bitcast.43), kind=kOutput, calls=%fused_computation.13 | convolution fusion | flops 7372800 | bytes 2556204 | tf_op jit(solution)/shard_map/eh,eha->ea/dot_general | solution.py:510
  171.6 0.0 copy-done.2
  171.6 0.7 fusion.3
  172.4 0.0 copy-done.5
  172.4 0.7 copy.27
Async XLA Ops:
  0.6 1.6 copy-start
  0.6 5.1 %copy-start.6 = (f32[3,25,25]{2,1,0:T(8,128)S(1)}, f32[3,25,25]{2,1,0:T(8,128)}, u32[]{:S(2)}) copy-start(f32[3,25,25]{2,1,0:T(8,128)} %param.22) | copy-start | bytes 22504
  5.7 3.1 %copy-start.9 = (f32[3,25]{1,0:T(4,128)S(1)}, f32[3,25]{1,0:T(4,128)}, u32[]{:S(2)}) copy-start(f32[3,25]{1,0:T(4,128)} %param.23) | copy-start | bytes 904
  8.8 2.1 %copy-start.1 = (s32[8192]{0:T(1024)S(1)}, s32[8192]{0:T(1024)}, u32[]{:S(2)}) copy-start(s32[8192]{0:T(1024)} %param.18) | copy-start | bytes 98308
  8.8 2.8 %copy-start.3 = (s32[3,8192]{1,0:T(4,128)S(1)}, s32[3,8192]{1,0:T(4,128)}, u32[]{:S(2)}) copy-start(s32[3,8192]{1,0:T(4,128)} %param.20) | copy-start | bytes 294916
  8.8 3.5 %copy-start.4 = (f32[3,8192]{1,0:T(4,128)S(1)}, f32[3,8192]{1,0:T(4,128)}, u32[]{:S(2)}) copy-start(f32[3,8192]{1,0:T(4,128)} %param.19) | copy-start | bytes 294916
  8.8 157.8 %copy-start.7 = (f32[3,25,64]{2,1,0:T(8,128)S(1)}, f32[3,25,64]{2,1,0:T(8,128)}, u32[]{:S(2)}) copy-start(f32[3,25,64]{2,1,0:T(8,128)} %param.25) | copy-start | bytes 57604
  8.8 157.8 %copy-start.8 = (f32[3,25]{1,0:T(4,128)S(1)}, f32[3,25]{1,0:T(4,128)}, u32[]{:S(2)}) copy-start(f32[3,25]{1,0:T(4,128)} %param.26) | copy-start | bytes 904
  13.6 156.0 %copy-start.10 = (f32[3,25]{1,0:T(4,128)S(1)}, f32[3,25]{1,0:T(4,128)}, u32[]{:S(2)}) copy-start(f32[3,25]{1,0:T(4,128)} %param.27) | copy-start | bytes 904
  166.6 5.0 %copy-start.2 = (f32[2,4,8,128]{3,1,2,0:T(4,128)}, f32[2,4,8,128]{3,1,2,0:T(4,128)S(1)}, u32[]{:S(2)}) copy-start(f32[2,4,8,128]{3,1,2,0:T(4,128)S(1)} %copy.26) | copy-start | bytes 98308
  166.7 5.7 %copy-start.5 = (f32[3,16,512]{2,1,0:T(8,128)S(1)}, f32[3,16,512]{2,1,0:T(8,128)}, u32[]{:S(2)}) copy-start(f32[3,16,512]{2,1,0:T(8,128)} %get-tuple-element.6) | copy-start | bytes 294916

commit v2 on v1

--- a/solution.py
+++ b/solution.py
@@ -142,13 +142,15 @@
 
 
 def kernel(
-    chi_ref, types_ref, offs_ref, base_ref, hard_ref,
+    desc_ref, types1_ref, offs1_ref, base1_ref, hard_ref,
+    wf_ref, ws_ref, wo_ref, sf_ref, sc_ref, so_ref,
     hx_ref, hxt_ref, hp_ref, hq_ref, hqt_ref, lanes_ref,
-    charges_ref, forces_ref,
+    out_charges_ref, out_forces_ref, out_short_ref,
     w_ref, s_ref, mx_ref, mp_ref, mq_ref, a_ref, b_ref, acc_ref,
     ones_ref, sp_ref, sd_ref, r1_ref, k1_ref, r2_ref, x2_ref, m_ref, r3_ref, green_ref,
     z3_ref, r3b_ref, k3b_ref, m2b_ref, r2b_ref, v1_ref, r1b_ref, phi0_ref, phi_ref,
     image_ref, p0_ref, d1_ref, t_ref, arx_ref, arp_ref, arq_ref, ars_ref,
+    types_ref, offs_ref, base_ref, chi_ref, charges_ref, pre_ref, n1_ref, n2_ref, n3_ref, tall_ref,
     send, recv,
 ):
     ix, ip, iq = lax.axis_index(GX), lax.axis_index(PAX), lax.axis_index(QAX)
@@ -157,6 +159,53 @@
     barrier = pltpu.get_barrier_semaphore()
     for _, where, _ in to_xq + to_p:
         pl.semaphore_signal(barrier, inc=1, device_id=where, device_id_type=MESH)
+
+    def part(c):
+        return pl.ds(c * CH, CH)
+
+    for c in range(NCH):
+        types_ref[c : c + 1, :] = types1_ref[:, c * CH : c * CH + CH]
+        for d in range(3):
+            offs_ref[d, c : c + 1, :] = offs1_ref[d : d + 1, c * CH : c * CH + CH]
+            base_ref[d, c : c + 1, :] = base1_ref[d : d + 1, c * CH : c * CH + CH]
+
+    n1_ref[...] = jnp.zeros(n1_ref.shape, F32)
+    n2_ref[...] = jnp.zeros(n2_ref.shape, F32)
+    n3_ref[...] = jnp.zeros(n3_ref.shape, F32)
+    tall_ref[...] = jnp.zeros(tall_ref.shape, F32)
+    for e in range(3):
+        n1_ref[32 * e : 32 * e + 25, :] = wf_ref[e]
+        n1_ref[96 + 32 * e : 96 + 32 * e + 25, :] = sf_ref[e]
+        n2_ref[32 * e : 32 * e + 25, 0:25] = ws_ref[e]
+    n3_ref[0:3, 0:25] = wo_ref[...]
+    n3_ref[8:11, 0:25] = so_ref[...]
+    tall_ref[0:3, 0:25] = sc_ref[...]
+    tall_ref[...] = jnp.transpose(tall_ref[...])
+    first_layer, second_layer = split(n1_ref[...]), split(n2_ref[...])
+    last_layer, short_layer = split(n3_ref[0:8, :]), split(n3_ref[8:16, :])
+
+    def by_type(c, first, second, third):
+        kind = types_ref[pl.ds(c, 1), :]
+        return jnp.where(kind == 0, first, jnp.where(kind == 1, second, third))
+
+    def net_start(c, carry):
+        pre = dot3(first_layer, desc_ref[:, part(c)])
+        pre_ref[c] = by_type(c, pre[96:128], pre[128:160], pre[160:192])
+        hidden = jnp.tanh(by_type(c, pre[0:32], pre[32:64], pre[64:96]))
+        pre = dot3(second_layer, hidden)
+        hidden = jnp.tanh(by_type(c, pre[0:32], pre[32:64], pre[64:96]))
+        value = dot3(last_layer, hidden)
+        chi_ref[pl.ds(c, 1), :] = by_type(c, value[0:1], value[1:2], value[2:3])
+        return carry
+
+    def net_end(c, carry):
+        charge = charges_ref[pl.ds(c, 1), :]
+        weight = by_type(c, tall_ref[0:32, 0:1], tall_ref[0:32, 1:2], tall_ref[0:32, 2:3])
+        hidden = jnp.tanh(pre_ref[c] + weight * charge)
+        value = dot3(short_layer, hidden)
+        out_short_ref[:, part(c)] = by_type(c, value[0:1], value[1:2], value[2:3])
+        out_charges_ref[:, part(c)] = charge
+        return carry
 
     hardness = jnp.where(
         types_ref[...] == 0, hard_ref[0], jnp.where(types_ref[...] == 1, hard_ref[1], hard_ref[2])
@@ -261,7 +310,7 @@
         wait_all(copies)
         return jnp.sum((arx_ref, arp_ref, arq_ref)[phase][...], axis=0)
 
-    def solve():
+    def solve(local_sums=None):
         r1_ref[ix] = sd_ref[ix, 0:XR, :]
         copies = send_all(to_x, lambda g: sd_ref.at[g, 0:XR], r1_ref.at[ix], send, recv, 0)
         wait_all(copies)
@@ -286,13 +335,17 @@
             to_xq, lambda n: m_ref.at[:, rows8(8 * n)], r3_ref.at[:, rows8(8 * mine)], send, recv, 12
         )
         wait_all(copies)
-        k3 = dot3(hq_ref, jnp.concatenate([r3_ref[0], r3_ref[1]], axis=1)) * green_ref[...]
+        k3 = dot3(hq_ref, jnp.concatenate([r3_ref[0], r3_ref[1]], axis=1))
+        energy_density = k3 * k3 * green_ref[...]
+        k3 = k3 * green_ref[...]
         z3 = dot3(hqt_ref, k3)
         z3_ref[0], z3_ref[1] = z3[:, 0:128], z3[:, 128:256]
         r3b_ref[:, rows8(8 * mine), :] = z3_ref[:, rows8(8 * mine), :]
         copies = send_all(
             to_xq, lambda n: z3_ref.at[:, rows8(8 * n)], r3b_ref.at[:, rows8(8 * mine)], send, recv, 44
         )
+        if local_sums is not None:
+            sums = ar_start(0, pack(local_sums(total(energy_density))))
         wait_all(copies)
         loaded = [
             jnp.concatenate([r3b_ref[h, pl.ds(y, 32, stride=8), :] for h in range(2)], axis=1)
@@ -311,11 +364,16 @@
             )
         r2b_ref[ip] = m2b_ref[ip]
         copies = send_all(to_p, lambda s: m2b_ref.at[s], r2b_ref.at[ip], send, recv, 76)
+        if local_sums is not None:
+            sums = ar_start(1, ar_done(0, sums))
         wait_all(copies)
         v1_ref[...] = dot3(hxt_ref, r2b_ref[...].reshape(M, LN)).reshape(4, XR, LN)
         r1b_ref[ix, 0:XR, :] = v1_ref[ix]
         copies = send_all(to_x, lambda g: v1_ref.at[g], r1b_ref.at[ix, 0:XR], send, recv, 84)
-        wait_all(copies)
+        if local_sums is not None:
+            sums = ar_start(2, ar_done(1, sums))
+        wait_all(copies)
+        return None if local_sums is None else ar_done(2, sums)
 
     def load_field(get):
         for g in range(4):
@@ -360,15 +418,15 @@
                 along_p = along_p + fold(block * s_p) * m_q
                 along_x = along_x + fold(t_ref[1, 32 * q : 32 * q + 32, :] * m_p) * m_q
             minus = -charges_ref[pl.ds(c, 1), :]
-            forces_ref[0, pl.ds(c, 1), :] = minus * jnp.sum(along_x, axis=0, keepdims=True)
-            forces_ref[P_DIM, pl.ds(c, 1), :] = minus * jnp.sum(along_p, axis=0, keepdims=True)
-            forces_ref[Q_DIM, pl.ds(c, 1), :] = minus * jnp.sum(along_q, axis=0, keepdims=True)
+            for d, along in ((0, along_x), (P_DIM, along_p), (Q_DIM, along_q)):
+                out_forces_ref[d : d + 1, part(c)] = minus * jnp.sum(along, axis=0, keepdims=True)
             return carry
 
         lax.fori_loop(0, NCH, step, 0)
 
     atoms = float(ATOMS * 256)
     clear(256)
+    lax.fori_loop(0, NCH, net_start, 0)
     chi = chi_ref[...]
     local_sum = total(chi)
     shift = local_sum * (1.0 / ATOMS)
@@ -425,22 +483,20 @@
             + (alpha0 * (image_mean - shift2)) * ones_ref[g]
             - alpha0 * (turned[0:64] + turned[64:128])
         )
-    solve()
-    load_field(lambda g: r1b_ref[g])
-    sample_image(d1_ref)
     d1 = d1_ref[...]
-    sums = pack([total(residual * residual), total(d1 * image_ref[...])])
-    copies = ar_start(0, sums)
-    copies = ar_start(1, ar_done(0, copies))
-    copies = ar_start(2, ar_done(1, copies))
-    sums = ar_done(2, copies)
+    sums = solve(lambda energy: [total(residual * residual), total(hardness * d1 * d1) + energy])
+    d1 = d1_ref[...]
     alpha1 = sums[0:1, 0:1] / sums[0:1, 1:2]
     charges_ref[...] = alpha0 * p0_ref[...] + alpha1 * d1
+    lax.fori_loop(0, NCH, net_end, 0)
     load_field(lambda g: alpha0 * phi0_ref[g] + alpha1 * r1b_ref[g])
     sample_forces()
 
 
-def equilibrate(chi, types, offsets, stencil_base, hardness):
+def per_device(
+    descriptors, types, offsets, stencil_base, w_first, w_second, w_out, hardness,
+    sr_first, sr_charge, sr_out,
+):
     tabs = tables()
     vmem = pl.BlockSpec(memory_space=pltpu.VMEM)
     smem = pl.BlockSpec(memory_space=pltpu.SMEM)
@@ -448,14 +504,15 @@
     def held(*shape, dtype=F32):
         return pltpu.VMEM(shape, dtype)
 
-    return pl.pallas_call(
+    charges, forces, short_energy = pl.pallas_call(
         kernel,
         out_shape=(
-            jax.ShapeDtypeStruct((NCH, CH), F32),
-            jax.ShapeDtypeStruct((3, NCH, CH), F32),
+            jax.ShapeDtypeStruct((1, ATOMS), F32),
+            jax.ShapeDtypeStruct((3, ATOMS), F32),
+            jax.ShapeDtypeStruct((1, ATOMS), F32),
         ),
-        in_specs=[vmem] * 4 + [smem] + [vmem] * 6,
-        out_specs=(vmem, vmem),
+        in_specs=[vmem] * 4 + [smem] + [vmem] * 12,
+        out_specs=(vmem, vmem, vmem),
         scratch_shapes=[
             held(3, 5, NCH, CH), held(3, 5, NCH, CH),
             held(NCH, 64, CH), held(NCH, 32, CH), held(NCH, 32, CH),
@@ -470,6 +527,9 @@
             held(NCH, CH), held(NCH, CH), held(NCH, CH),
             held(2, 896, CH),
             held(4, 8, 128), held(8, 8, 128), held(8, 8, 128), held(3, 8, 128),
+            held(NCH, CH, dtype=jnp.int32), held(3, NCH, CH), held(3, NCH, CH, dtype=jnp.int32),
+            held(NCH, CH), held(NCH, CH), held(NCH, 32, CH),
+            held(192, 64), held(96, 32), held(16, 32), held(128, 128),
             pltpu.SemaphoreType.DMA((120,)),
             pltpu.SemaphoreType.DMA((120,)),
         ],
@@ -478,38 +538,11 @@
         ),
         name="equilibrate",
     )(
-        chi.reshape(NCH, CH), types.reshape(NCH, CH), offsets.reshape(3, NCH, CH),
-        stencil_base.reshape(3, NCH, CH), hardness, *[jnp.asarray(t) for t in tabs],
+        descriptors, types.reshape(1, ATOMS), offsets, stencil_base, hardness,
+        w_first, w_second, w_out, sr_first, sr_charge, sr_out,
+        *[jnp.asarray(t) for t in tabs],
     )
-
-
-def element_net(first, second, final, descriptors, onehot):
-    hidden = jnp.tanh(
-        jnp.einsum("ehf,fa->eha", first, descriptors, precision=lax.Precision.HIGHEST)
-    )
-    hidden = jnp.tanh(jnp.einsum("ehg,ega->eha", second, hidden, precision=lax.Precision.HIGHEST))
-    output = jnp.einsum("eh,eha->ea", final, hidden, precision=lax.Precision.HIGHEST)
-    return jnp.sum(onehot * output, axis=0)
-
-
-def per_device(
-    descriptors, types, offsets, stencil_base, w_first, w_second, w_out, hardness,
-    sr_first, sr_charge, sr_out,
-):
-    elements = w_first.shape[0]
-    onehot = (types[None, :] == jnp.arange(elements, dtype=jnp.int32)[:, None]).astype(F32)
-    chi = element_net(w_first, w_second, w_out, descriptors, onehot)
-    charges, forces = equilibrate(chi, types, offsets, stencil_base, hardness)
-    charges = charges.reshape(ATOMS)
-    forces = forces.reshape(3, ATOMS)
-    hidden = jnp.tanh(
-        jnp.einsum("ehf,fa->eha", sr_first, descriptors, precision=lax.Precision.HIGHEST)
-        + sr_charge[:, :, None] * charges[None, None, :]
-    )
-    short_energy = jnp.sum(
-        onehot * jnp.einsum("eh,eha->ea", sr_out, hidden, precision=lax.Precision.HIGHEST), axis=0
-    )
-    return charges, forces, short_energy
+    return charges.reshape(ATOMS), forces, short_energy.reshape(ATOMS)
 
 
 def solution(mesh):

time: 173 us -> 153 us (0.88)
  matrix products: 13.4 us -> 0 us
  Pallas kernels: 152 us -> 148 us
    dot_general x5 -> x0, matrix products: 13.4 us -> none  [the longest x1 3.48 us: element_net(): jnp.einsum('ehf,fa->eha', first, descriptors, precision=lax.Precision.HIG...]
    pallas_call x1, Pallas kernels: 152 us -> 148 us  [per_device(): pl.pallas_call(kernel, out_shape=(jax.ShapeDtypeStruct((1, ATOMS), F32),...]
    unnamed x26 -> x3, local copies, waits for them, and re-layouts: 4.47 us -> 4.33 us
where the time goes in v2:
time: 153 us
  Pallas kernels  148 us (97%)
  local copies, waits for them, and re-layouts  4.33 us (3%)
    pallas_call x1, Pallas kernels, per_device(): pl.pallas_call(kernel, out_shape=(jax.ShapeDtypeStruct((1, ATOMS), F32),...  148 us
    unnamed x3, local copies, waits for them, and re-layouts  4.33 us

profile of v2, /device:TPU:1, one launch (start us, length us, event | category | flops | bytes accessed | tf_op | source)
XLA Modules:
  0.0 152.9 jit_solution(15329196534097931959)
XLA Ops:
  0.6 148.0 %equilibrate.1 = (f32[1,8192]{1,0:T(1,128)}, f32[3,8192]{1,0:T(4,128)}, f32[1,8192]{1,0:T(1,128)}) custom-call(f32[64,8192]{1,0:T(8,128)} %desc_ref.1, s32[1,8192]{1,0:T(1,128)} %bitcast.3, f32[3,8192]{1,0:T(4,128)} %offs1_ref.1, s32[3,8192]{1,0:T(4,128)} %base1_ref.1, f32[3]{0:T(128)} %hard_ref.1, f32[3,25,64]{2,1,0:T(8,128)} %wf_ref.1, ...), custom_call_target="tpu_custom_call" | custom-call | tf_op jit(solution)/shard_map/equilibrate/pallas_call | solution.py:507
  148.6 1.4 copy.23
  150.0 1.6 %copy.24 = f32[3,8192]{1,0:T(4,128)} copy(f32[3,8192]{1,0:T(4,128)} %get-tuple-element.13) | data formatting | bytes 196608
  151.6 1.4 copy.25

commit v3 on v2

--- a/solution.py
+++ b/solution.py
@@ -11,12 +11,14 @@
 
 M = 192
 SMEAR = 0.75
-GX, PAX, QAX = "gx", "gy", "gz"
-P_DIM, Q_DIM = 1, 2
+GX, PAX, QAX = "gx", "gz", "gy"
+P_DIM, Q_DIM = 2, 1
 AXES = ("gx", "gy", "gz")
 ATOMS = 8192
 CH = 512
 NCH = ATOMS // CH
+PAIRS = NCH // 2
+WIDE = 2048
 XR = 56
 LN = 256
 F32, BF16 = jnp.float32, jnp.bfloat16
@@ -125,19 +127,26 @@
     return pl.ds(pl.multiple_of(start, 8), 8)
 
 
-def comb_store(ref, row, value):
-    for h in range(2):
-        ref[h, pl.ds(row, 32, stride=8), :] = value[:, 128 * h : 128 * h + 128]
-
-
-def lane_pick(pieces, width, length=LN):
+def comb(row):
+    return pl.ds(row, 32, stride=8)
+
+
+def turn(value, shift):
+    shift = shift % value.shape[1]
+    return value if shift == 0 else pltpu.roll(value, shift, 1)
+
+
+def waits(copies):
+    for copy in copies:
+        copy.wait_recv()
+
+
+def lane_pick(pieces, width):
     lane = lax.broadcasted_iota(jnp.int32, pieces[0][0].shape, 1)
     result = jnp.zeros(pieces[0][0].shape, F32)
     for number, (array, shift) in enumerate(pieces):
-        shift = shift % length
-        moved = array if shift == 0 else pltpu.roll(array, shift, 1)
         inside = (lane >= number * width) & (lane < (number + 1) * width)
-        result = jnp.where(inside, moved, result)
+        result = jnp.where(inside, turn(array, shift), result)
     return result
 
 
@@ -146,9 +155,10 @@
     wf_ref, ws_ref, wo_ref, sf_ref, sc_ref, so_ref,
     hx_ref, hxt_ref, hp_ref, hq_ref, hqt_ref, lanes_ref,
     out_charges_ref, out_forces_ref, out_short_ref,
-    w_ref, s_ref, mx_ref, mp_ref, mq_ref, a_ref, b_ref, acc_ref,
-    ones_ref, sp_ref, sd_ref, r1_ref, k1_ref, r2_ref, x2_ref, m_ref, r3_ref, green_ref,
-    z3_ref, r3b_ref, k3b_ref, m2b_ref, r2b_ref, v1_ref, r1b_ref, phi0_ref, phi_ref,
+    w_ref, s_ref, mx_ref, mp_ref, mq_ref, bx_ref, sx_ref, sp_mask_ref, sq_mask_ref,
+    a0_ref, a1_ref, b0_ref, b1_ref, acc_ref,
+    ones_ref, sp_ref, sd_ref, r1_ref, k1_ref, r2_ref, x2_ref, m_ref, r3_ref, r3x_ref, green_ref,
+    z3_ref, z3x_ref, r3b_ref, k3b_ref, m2b_ref, r2b_ref, v1_ref, r1b_ref, phi0_ref, phi_ref,
     image_ref, p0_ref, d1_ref, t_ref, arx_ref, arp_ref, arq_ref, ars_ref,
     types_ref, offs_ref, base_ref, chi_ref, charges_ref, pre_ref, n1_ref, n2_ref, n3_ref, tall_ref,
     send, recv,
@@ -184,27 +194,40 @@
     first_layer, second_layer = split(n1_ref[...]), split(n2_ref[...])
     last_layer, short_layer = split(n3_ref[0:8, :]), split(n3_ref[8:16, :])
 
-    def by_type(c, first, second, third):
-        kind = types_ref[pl.ds(c, 1), :]
+    def wide(i):
+        return pl.ds(i * WIDE, WIDE)
+
+    def by_type(i, first, second, third):
+        kind = types1_ref[:, wide(i)]
         return jnp.where(kind == 0, first, jnp.where(kind == 1, second, third))
 
-    def net_start(c, carry):
-        pre = dot3(first_layer, desc_ref[:, part(c)])
-        pre_ref[c] = by_type(c, pre[96:128], pre[128:160], pre[160:192])
-        hidden = jnp.tanh(by_type(c, pre[0:32], pre[32:64], pre[64:96]))
+    def net_chi(i, carry):
+        pre = dot3([half[0:96] for half in first_layer], desc_ref[:, wide(i)])
+        hidden = jnp.tanh(by_type(i, pre[0:32], pre[32:64], pre[64:96]))
         pre = dot3(second_layer, hidden)
-        hidden = jnp.tanh(by_type(c, pre[0:32], pre[32:64], pre[64:96]))
+        hidden = jnp.tanh(by_type(i, pre[0:32], pre[32:64], pre[64:96]))
         value = dot3(last_layer, hidden)
-        chi_ref[pl.ds(c, 1), :] = by_type(c, value[0:1], value[1:2], value[2:3])
+        value = by_type(i, value[0:1], value[1:2], value[2:3])
+        for k in range(WIDE // CH):
+            chi_ref[pl.ds(WIDE // CH * i + k, 1), :] = value[:, CH * k : CH * k + CH]
         return carry
 
-    def net_end(c, carry):
-        charge = charges_ref[pl.ds(c, 1), :]
-        weight = by_type(c, tall_ref[0:32, 0:1], tall_ref[0:32, 1:2], tall_ref[0:32, 2:3])
-        hidden = jnp.tanh(pre_ref[c] + weight * charge)
+    def net_short(i, carry):
+        pre = dot3([half[96:192] for half in first_layer], desc_ref[:, wide(i)])
+        pre_ref[:, wide(i)] = by_type(i, pre[0:32], pre[32:64], pre[64:96])
+        return carry
+
+    def net_end(i, carry):
+        rows = [charges_ref[pl.ds(WIDE // CH * i + k, 1), :] for k in range(WIDE // CH)]
+        charge = jnp.concatenate(rows, axis=1)
+        weight = by_type(i, tall_ref[0:32, 0:1], tall_ref[0:32, 1:2], tall_ref[0:32, 2:3])
+        hidden = jnp.tanh(pre_ref[:, wide(i)] + weight * charge)
         value = dot3(short_layer, hidden)
-        out_short_ref[:, part(c)] = by_type(c, value[0:1], value[1:2], value[2:3])
-        out_charges_ref[:, part(c)] = charge
+        value = by_type(i, value[0:1], value[1:2], value[2:3])
+        for k in range(WIDE // 128):
+            row = pl.ds(WIDE // 128 * i + k, 1)
+            out_short_ref[row, :] = value[:, 128 * k : 128 * k + 128]
+            out_charges_ref[row, :] = charge[:, 128 * k : 128 * k + 128]
         return carry
 
     hardness = jnp.where(
@@ -244,12 +267,12 @@
         wave > 0, (4.0 * math.pi / (M * M * M)) * jnp.exp((-0.5 * SMEAR * SMEAR) * wave) / safe, 0.0
     )
 
-    zero8 = jnp.zeros((8, LN), F32)
     for g in range(4):
-        r1b_ref[g, XR : XR + 8, :] = zero8
+        for h in range(2):
+            r1b_ref[h, g, XR : XR + 8, :] = jnp.zeros((8, 128), F32)
         acc_ref[256 * g + 224 : 256 * g + 256, :] = jnp.zeros((32, 256), F32)
     x2_ref[168:256, :] = jnp.zeros((88, LN), F32)
-    comb_store(m_ref, 7, jnp.zeros((32, LN), F32))
+    r3x_ref[comb(7), :] = jnp.zeros((32, 128), F32)
     k3b_ref[192:256, :] = jnp.zeros((64, LN), F32)
 
     def mask(table, d, c, count):
@@ -260,25 +283,52 @@
             result = jnp.where(place == j, table[d, j, pl.ds(c, 1), :], result)
         return result
 
-    def spread(values_ref, shift, lo, hi, first):
-        def step(c, carry):
-            if first:
-                m_x, m_p, m_q = mask(w_ref, 0, c, 64), mask(w_ref, P_DIM, c, 32), mask(w_ref, Q_DIM, c, 32)
-                mx_ref[c], mp_ref[c], mq_ref[c] = m_x, m_p, m_q
-                for q in range(28):
-                    high, low = split(m_p * m_q[q : q + 1, :])
-                    a_ref[c, 32 * q : 32 * q + 32, :] = high
-                    a_ref[c, 896 + 32 * q : 896 + 32 * q + 32, :] = low
-                b_ref[128:192, :], b_ref[192:256, :] = split(m_x)
-            else:
-                m_x = mx_ref[c]
-            b_ref[0:64, :], b_ref[64:128, :] = split(m_x * (values_ref[pl.ds(c, 1), :] - shift))
-            width = 256 if first else 128
-            part = dot(a_ref[c], b_ref[0:width, :], ((1,), (1,)))
-            for g in range(4):
-                acc_ref[256 * g : 256 * g + 224, 0:width] += (
-                    part[224 * g : 224 * g + 224] + part[896 + 224 * g : 896 + 224 * g + 224]
-                )
+    def slope_masks(c, carry):
+        high, low = split(mask(s_ref, 0, c, 64))
+        sx_ref[c, 0:64, :], sx_ref[c, 64:128, :] = high, low
+        sp_mask_ref[c], sq_mask_ref[c] = mask(s_ref, P_DIM, c, 32), mask(s_ref, Q_DIM, c, 32)
+        return carry
+
+    def build(c, a_ref, i, b_ref, values_ref, shift):
+        m_x, m_p, m_q = mask(w_ref, 0, c, 64), mask(w_ref, P_DIM, c, 32), mask(w_ref, Q_DIM, c, 32)
+        mx_ref[c], mp_ref[c], mq_ref[c] = m_x, m_p, m_q
+        for q in range(28):
+            high, low = split(m_p * m_q[q : q + 1, :])
+            a_ref[i, 32 * q : 32 * q + 32, :] = high
+            a_ref[i, 896 + 32 * q : 896 + 32 * q + 32, :] = low
+        high, low = split(m_x)
+        b_ref[128:192, :], b_ref[192:256, :] = high, low
+        bx_ref[c, 0:64, :], bx_ref[c, 64:128, :] = high, low
+        b_ref[0:64, :], b_ref[64:128, :] = split(m_x * (values_ref[pl.ds(c, 1), :] - shift))
+
+    def gather_part(part, width):
+        for g in range(4):
+            acc_ref[256 * g : 256 * g + 224, 0:width] += (
+                part[224 * g : 224 * g + 224] + part[896 + 224 * g : 896 + 224 * g + 224]
+            )
+
+    def spread_first(lo, hi):
+        def step(i, carry):
+            part = dot(a0_ref[i], b0_ref[...], ((1,), (1,)))
+            build(2 * i + 1, a1_ref, i, b1_ref, chi_ref, shift)
+            gather_part(part, 256)
+            part = dot(a1_ref[i], b1_ref[...], ((1,), (1,)))
+            after = lax.rem(i + 1, PAIRS)
+            build(2 * after, a0_ref, after, b0_ref, chi_ref, shift)
+            gather_part(part, 256)
+            return carry
+
+        lax.fori_loop(lo, hi, step, 0)
+
+    def spread_image(lo, hi):
+        def step(i, carry):
+            for c, b_ref in ((2 * i, b0_ref), (2 * i + 1, b1_ref)):
+                value = image_ref[pl.ds(c, 1), :] - shift2
+                b_ref[0:64, :], b_ref[64:128, :] = split(mx_ref[c] * value)
+            part = dot(a0_ref[i], b0_ref[0:128, :], ((1,), (1,)))
+            other = dot(a1_ref[i], b1_ref[0:128, :], ((1,), (1,)))
+            gather_part(part, 128)
+            gather_part(other, 128)
             return carry
 
         lax.fori_loop(lo, hi, step, 0)
@@ -300,7 +350,7 @@
 
     def ar_start(phase, tile):
         peers, slots, me, base = (
-            (to_x, arx_ref, ix, 100), (to_p, arp_ref, ip, 104), (to_q, arq_ref, iq, 112)
+            (to_x, arx_ref, ix, 112), (to_p, arp_ref, ip, 116), (to_q, arq_ref, iq, 124)
         )[phase]
         slots[me] = tile
         ars_ref[phase] = tile
@@ -310,46 +360,72 @@
         wait_all(copies)
         return jnp.sum((arx_ref, arp_ref, arq_ref)[phase][...], axis=0)
 
-    def solve(local_sums=None):
-        r1_ref[ix] = sd_ref[ix, 0:XR, :]
-        copies = send_all(to_x, lambda g: sd_ref.at[g, 0:XR], r1_ref.at[ix], send, recv, 0)
-        wait_all(copies)
-        k1 = dot3(hx_ref, r1_ref[...].reshape(4 * XR, LN))
-        k1_ref[...] = k1.reshape(8, 24, LN)
-        r2_ref[ip] = k1_ref[ip]
-        copies = send_all(to_p, lambda s: k1_ref.at[s], r2_ref.at[ip], send, recv, 4)
-        wait_all(copies)
+    def solve(local_sums=None, during=()):
+        halves_of = [slice(0, 128), slice(128, 256)]
+        to_wait = []
+        for h, lanes in enumerate(halves_of):
+            r1_ref[h, ix] = sd_ref[ix, 0:XR, lanes]
+            to_wait.append(
+                send_all(to_x, lambda g: sd_ref.at[g, 0:XR, lanes], r1_ref.at[h, ix], send, recv, 4 * h)
+            )
+        if during:
+            during[0]()
+        moved = []
+        for h in range(2):
+            waits(to_wait[h])
+            k1_ref[h] = dot3(hx_ref, r1_ref[h].reshape(4 * XR, 128)).reshape(8, 24, 128)
+            r2_ref[h, ip] = k1_ref[h, ip]
+            moved.append(
+                send_all(to_p, lambda s: k1_ref.at[h, s], r2_ref.at[h, ip], send, recv, 8 + 8 * h)
+            )
+        if during:
+            during[1]()
+        to_wait += moved
+        for h in range(2):
+            waits(moved[h])
+            for y in range(4 * h, min(4 * h + 4, 7)):
+                for side in range(2):
+                    x2_ref[24 * y : 24 * y + 24, 128 * side : 128 * side + 128] = lane_pick(
+                        [(r2_ref[h, 4 * side + s], 32 * (s - y)) for s in range(4)], 32
+                    )
+        k2 = dot3((hp_ref[0, 0:M, :], hp_ref[1, 0:M, :]), x2_ref[...], ((1,), (1,)))
+        lane = lax.broadcasted_iota(jnp.int32, (32, 128), 1)
+        rest = jnp.zeros((32, 128), F32)
         for y in range(7):
-            x2_ref[24 * y : 24 * y + 24, :] = lane_pick(
-                [(r2_ref[s], 32 * (s - y)) for s in range(8)], 32
-            )
-        k2 = dot3((hp_ref[0, 0:M, :], hp_ref[1, 0:M, :]), x2_ref[...], ((1,), (1,)))
+            block = lane_pick([(k2[32 * k : 32 * k + 32, :], 24 * (k - y)) for k in range(6)], 24)
+            m_ref[comb(y), :] = block[:, 0:128]
+            rest = jnp.where((lane >= 16 * y) & (lane < 16 * y + 16), turn(block[:, 128:256], 16 * y), rest)
+        m_ref[comb(7), :] = rest
+        r3_ref[rows8(8 * mine), :] = m_ref[rows8(8 * mine), :]
+        copies = send_all(
+            to_xq, lambda n: m_ref.at[rows8(8 * n)], r3_ref.at[rows8(8 * mine)], send, recv, 24
+        )
+        to_wait.append(copies)
+        waits(copies)
+        rest = r3_ref[comb(7), :]
         for y in range(7):
-            comb_store(
-                m_ref,
-                y,
-                lane_pick([(k2[32 * k : 32 * k + 32, :], 24 * (k - y)) for k in range(6)], 24),
-            )
-        r3_ref[:, rows8(8 * mine), :] = m_ref[:, rows8(8 * mine), :]
-        copies = send_all(
-            to_xq, lambda n: m_ref.at[:, rows8(8 * n)], r3_ref.at[:, rows8(8 * mine)], send, recv, 12
-        )
-        wait_all(copies)
-        k3 = dot3(hq_ref, jnp.concatenate([r3_ref[0], r3_ref[1]], axis=1))
+            r3x_ref[comb(y), :] = jnp.where(lane < 16, turn(rest, -16 * y), 0.0)
+        k3 = dot3(hq_ref, jnp.concatenate([r3_ref[...], r3x_ref[...]], axis=1))
         energy_density = k3 * k3 * green_ref[...]
         k3 = k3 * green_ref[...]
         z3 = dot3(hqt_ref, k3)
-        z3_ref[0], z3_ref[1] = z3[:, 0:128], z3[:, 128:256]
-        r3b_ref[:, rows8(8 * mine), :] = z3_ref[:, rows8(8 * mine), :]
+        z3_ref[...], z3x_ref[...] = z3[:, 0:128], z3[:, 128:256]
+        rest = jnp.zeros((32, 128), F32)
+        for y in range(7):
+            inside = (lane >= 16 * y) & (lane < 16 * y + 16)
+            rest = jnp.where(inside, turn(z3x_ref[comb(y), :], 16 * y), rest)
+        z3_ref[comb(7), :] = rest
+        r3b_ref[rows8(8 * mine), :] = z3_ref[rows8(8 * mine), :]
         copies = send_all(
-            to_xq, lambda n: z3_ref.at[:, rows8(8 * n)], r3b_ref.at[:, rows8(8 * mine)], send, recv, 44
+            to_xq, lambda n: z3_ref.at[rows8(8 * n)], r3b_ref.at[rows8(8 * mine)], send, recv, 56
         )
         if local_sums is not None:
             sums = ar_start(0, pack(local_sums(total(energy_density))))
-        wait_all(copies)
+        to_wait.append(copies)
+        waits(copies)
+        rest = r3b_ref[comb(7), :]
         loaded = [
-            jnp.concatenate([r3b_ref[h, pl.ds(y, 32, stride=8), :] for h in range(2)], axis=1)
-            for y in range(7)
+            jnp.concatenate([r3b_ref[comb(y), :], turn(rest, -16 * y)], axis=1) for y in range(7)
         ]
         for k in range(6):
             k3b_ref[32 * k : 32 * k + 32, :] = lane_pick(
@@ -358,22 +434,41 @@
         turned = jnp.transpose(k3b_ref[...])
         high, low = split(turned)
         v2 = dot(high, hp_ref[0]) + (dot(low, hp_ref[0]) + dot(high, hp_ref[1]))
-        for s in range(8):
-            m2b_ref[s] = lane_pick(
-                [(v2[24 * y : 24 * y + 24, :], 32 * (y - s)) for y in range(7)], 32
+        moved = []
+        for h in range(2):
+            for s in range(8):
+                lanes = halves_of[s // 4]
+                m2b_ref[h, s] = lane_pick(
+                    [(v2[24 * y : 24 * y + 24, lanes], 32 * (y - s)) for y in range(4 * h, min(4 * h + 4, 7))],
+                    32,
+                )
+            r2b_ref[h, ip] = m2b_ref[h, ip]
+            moved.append(
+                send_all(to_p, lambda s: m2b_ref.at[h, s], r2b_ref.at[h, ip], send, recv, 88 + 8 * h)
             )
-        r2b_ref[ip] = m2b_ref[ip]
-        copies = send_all(to_p, lambda s: m2b_ref.at[s], r2b_ref.at[ip], send, recv, 76)
         if local_sums is not None:
             sums = ar_start(1, ar_done(0, sums))
-        wait_all(copies)
-        v1_ref[...] = dot3(hxt_ref, r2b_ref[...].reshape(M, LN)).reshape(4, XR, LN)
-        r1b_ref[ix, 0:XR, :] = v1_ref[ix]
-        copies = send_all(to_x, lambda g: v1_ref.at[g], r1b_ref.at[ix, 0:XR], send, recv, 84)
+        to_wait += moved
+        back = []
+        for h in range(2):
+            waits(moved[h])
+            v1_ref[h] = dot3(hxt_ref, r2b_ref[h].reshape(M, 128)).reshape(4, XR, 128)
+            r1b_ref[h, ix, 0:XR, :] = v1_ref[h, ix]
+            back.append(
+                send_all(to_x, lambda g: v1_ref.at[h, g], r1b_ref.at[h, ix, 0:XR], send, recv, 104 + 4 * h)
+            )
         if local_sums is not None:
             sums = ar_start(2, ar_done(1, sums))
-        wait_all(copies)
+        to_wait += back
+        for copies in back:
+            waits(copies)
+        for copies in to_wait:
+            for copy in copies:
+                copy.wait_send()
         return None if local_sums is None else ar_done(2, sums)
+
+    def field(g):
+        return jnp.concatenate([r1b_ref[0, g], r1b_ref[1, g]], axis=1)
 
     def load_field(get):
         for g in range(4):
@@ -383,74 +478,89 @@
             phi_ref[224 * g : 224 * g + 224, 0:128] = turned
             phi_ref[224 * g : 224 * g + 224, 128:256] = turned
 
-    def x_contract(m_x, slot):
-        high, low = split(m_x)
-        b_ref[0:64, :], b_ref[64:128, :], b_ref[128:192, :], b_ref[192:256, :] = high, high, low, low
-        t_ref[slot] = dot(phi_ref[...], b_ref[...])
+    def x_contract(table, c, slot):
+        high, low = table[c, 0:64, :], table[c, 64:128, :]
+        t_ref[slot] = dot(phi_ref[...], jnp.concatenate([high, high, low, low], axis=0))
 
     def fold(product):
         return (product[0:8] + product[8:16]) + (product[16:24] + product[24:32])
 
+    def in_pairs(contract, reduce):
+        contract(0, 0)
+
+        def step(i, carry):
+            contract(2 * i + 1, 1)
+            reduce(2 * i, 0)
+            contract(2 * lax.rem(i + 1, PAIRS), 0)
+            reduce(2 * i + 1, 1)
+            return carry
+
+        lax.fori_loop(0, PAIRS, step, 0)
+
     def sample_image(values_ref):
-        def step(c, carry):
-            x_contract(mx_ref[c], 0)
+        def reduce(c, slot):
             m_p = mp_ref[c]
             found = jnp.zeros((8, CH), F32)
             for q in range(28):
-                found = found + fold(t_ref[0, 32 * q : 32 * q + 32, :] * m_p) * mq_ref[c, q : q + 1, :]
+                found = found + fold(t_ref[slot, 32 * q : 32 * q + 32, :] * m_p) * mq_ref[c, q : q + 1, :]
             image_ref[pl.ds(c, 1), :] = jnp.sum(found, axis=0, keepdims=True)
-            return carry
-
-        lax.fori_loop(0, NCH, step, 0)
+
+        in_pairs(lambda c, slot: x_contract(bx_ref, c, slot), reduce)
         image_ref[...] = image_ref[...] + hardness * values_ref[...]
 
     def sample_forces():
-        def step(c, carry):
-            m_p, s_p = mp_ref[c], mask(s_ref, P_DIM, c, 32)
-            b = mask(s_ref, Q_DIM, c, 32)
-            x_contract(mx_ref[c], 0)
-            x_contract(mask(s_ref, 0, c, 64), 1)
+        def contract(c, slot):
+            x_contract(bx_ref, c, slot)
+            x_contract(sx_ref, c, slot + 2)
+
+        def reduce(c, slot):
+            m_p, s_p = mp_ref[c], sp_mask_ref[c]
             along_x, along_p, along_q = (jnp.zeros((8, CH), F32) for _ in range(3))
             for q in range(28):
-                block = t_ref[0, 32 * q : 32 * q + 32, :]
+                block = t_ref[slot, 32 * q : 32 * q + 32, :]
                 m_q = mq_ref[c, q : q + 1, :]
-                along_q = along_q + fold(block * m_p) * b[q : q + 1, :]
+                along_q = along_q + fold(block * m_p) * sq_mask_ref[c, q : q + 1, :]
                 along_p = along_p + fold(block * s_p) * m_q
-                along_x = along_x + fold(t_ref[1, 32 * q : 32 * q + 32, :] * m_p) * m_q
+                along_x = along_x + fold(t_ref[slot + 2, 32 * q : 32 * q + 32, :] * m_p) * m_q
             minus = -charges_ref[pl.ds(c, 1), :]
             for d, along in ((0, along_x), (P_DIM, along_p), (Q_DIM, along_q)):
                 out_forces_ref[d : d + 1, part(c)] = minus * jnp.sum(along, axis=0, keepdims=True)
-            return carry
-
-        lax.fori_loop(0, NCH, step, 0)
+
+        in_pairs(contract, reduce)
 
     atoms = float(ATOMS * 256)
     clear(256)
-    lax.fori_loop(0, NCH, net_start, 0)
+    lax.fori_loop(0, ATOMS // WIDE, net_chi, 0)
     chi = chi_ref[...]
     local_sum = total(chi)
     shift = local_sum * (1.0 / ATOMS)
     pl.semaphore_wait(barrier, len(to_xq) + len(to_p))
     copies = ar_start(0, pack([local_sum]))
-    spread(chi_ref, shift, 0, 5, True)
+    build(0, a0_ref, 0, b0_ref, chi_ref, shift)
+    spread_first(0, 2)
     copies = ar_start(1, ar_done(0, copies))
-    spread(chi_ref, shift, 5, 11, True)
+    spread_first(2, 6)
     copies = ar_start(2, ar_done(1, copies))
-    spread(chi_ref, shift, 11, NCH, True)
+    spread_first(6, PAIRS)
     mean = ar_done(2, copies)[0:1, 0:1] * (1.0 / atoms)
     for g in range(4):
         turned = jnp.transpose(acc_ref[256 * g : 256 * g + 256, :])
         ones = turned[128:192] + turned[192:256]
         ones_ref[g] = ones
-        field = (mean - shift) * ones - (turned[0:64] + turned[64:128])
-        sp_ref[g] = field
-        sd_ref[g] = field
+        density = (mean - shift) * ones - (turned[0:64] + turned[64:128])
+        sp_ref[g] = density
+        sd_ref[g] = density
     p0 = mean - chi
     p0_ref[...] = p0
-    solve()
+    solve(
+        during=(
+            lambda: lax.fori_loop(0, ATOMS // WIDE, net_short, 0),
+            lambda: lax.fori_loop(0, NCH, slope_masks, 0),
+        )
+    )
     for g in range(4):
-        phi0_ref[g] = r1b_ref[g]
-    load_field(lambda g: r1b_ref[g])
+        phi0_ref[g] = field(g)
+    load_field(field)
     sample_image(p0_ref)
 
     image = image_ref[...]
@@ -459,11 +569,11 @@
     sums = pack([total(p0 * p0), total(p0 * image), image_sum, total(image * image), total(p0)])
     clear(128)
     copies = ar_start(0, sums)
-    spread(image_ref, shift2, 0, 5, False)
+    spread_image(0, 2)
     copies = ar_start(1, ar_done(0, copies))
-    spread(image_ref, shift2, 5, 11, False)
+    spread_image(2, 6)
     copies = ar_start(2, ar_done(1, copies))
-    spread(image_ref, shift2, 11, NCH, False)
+    spread_image(6, PAIRS)
     sums = ar_done(2, copies)
     norm0, curve0, image_total, image_square, p0_total = (sums[0:1, k : k + 1] for k in range(5))
     alpha0 = norm0 / curve0
@@ -488,8 +598,8 @@
     d1 = d1_ref[...]
     alpha1 = sums[0:1, 0:1] / sums[0:1, 1:2]
     charges_ref[...] = alpha0 * p0_ref[...] + alpha1 * d1
-    lax.fori_loop(0, NCH, net_end, 0)
-    load_field(lambda g: alpha0 * phi0_ref[g] + alpha1 * r1b_ref[g])
+    lax.fori_loop(0, ATOMS // WIDE, net_end, 0)
+    load_field(lambda g: alpha0 * phi0_ref[g] + alpha1 * field(g))
     sample_forces()
 
 
@@ -507,34 +617,37 @@
     charges, forces, short_energy = pl.pallas_call(
         kernel,
         out_shape=(
-            jax.ShapeDtypeStruct((1, ATOMS), F32),
+            jax.ShapeDtypeStruct((ATOMS // 128, 128), F32),
             jax.ShapeDtypeStruct((3, ATOMS), F32),
-            jax.ShapeDtypeStruct((1, ATOMS), F32),
+            jax.ShapeDtypeStruct((ATOMS // 128, 128), F32),
         ),
         in_specs=[vmem] * 4 + [smem] + [vmem] * 12,
         out_specs=(vmem, vmem, vmem),
         scratch_shapes=[
             held(3, 5, NCH, CH), held(3, 5, NCH, CH),
             held(NCH, 64, CH), held(NCH, 32, CH), held(NCH, 32, CH),
-            held(NCH, 1792, CH, dtype=BF16), held(256, CH, dtype=BF16),
+            held(NCH, 128, CH, dtype=BF16), held(NCH, 128, CH, dtype=BF16),
+            held(NCH, 32, CH), held(NCH, 32, CH),
+            held(PAIRS, 1792, CH, dtype=BF16), held(PAIRS, 1792, CH, dtype=BF16),
+            held(256, CH, dtype=BF16), held(256, CH, dtype=BF16),
             held(1024, 256),
             held(4, 64, LN), held(4, 64, LN), held(4, 64, LN),
-            held(4, XR, LN), held(8, 24, LN), held(8, 24, LN),
-            held(256, LN), held(2, 256, 128), held(2, 256, 128), held(M, LN),
-            held(2, 256, 128), held(2, 256, 128), held(256, LN),
-            held(8, 24, LN), held(8, 24, LN), held(4, XR, LN),
-            held(4, 64, LN), held(4, 64, LN), held(896, 256, dtype=BF16),
+            held(2, 4, XR, 128), held(2, 8, 24, 128), held(2, 8, 24, 128),
+            held(256, LN), held(256, 128), held(256, 128), held(256, 128), held(M, LN),
+            held(256, 128), held(256, 128), held(256, 128), held(256, LN),
+            held(2, 8, 24, 128), held(2, 8, 24, 128), held(2, 4, XR, 128),
+            held(2, 4, 64, 128), held(4, 64, LN), held(896, 256, dtype=BF16),
             held(NCH, CH), held(NCH, CH), held(NCH, CH),
-            held(2, 896, CH),
+            held(4, 896, CH),
             held(4, 8, 128), held(8, 8, 128), held(8, 8, 128), held(3, 8, 128),
             held(NCH, CH, dtype=jnp.int32), held(3, NCH, CH), held(3, NCH, CH, dtype=jnp.int32),
-            held(NCH, CH), held(NCH, CH), held(NCH, 32, CH),
+            held(NCH, CH), held(NCH, CH), held(32, ATOMS),
             held(192, 64), held(96, 32), held(16, 32), held(128, 128),
-            pltpu.SemaphoreType.DMA((120,)),
-            pltpu.SemaphoreType.DMA((120,)),
+            pltpu.SemaphoreType.DMA((132,)),
+            pltpu.SemaphoreType.DMA((132,)),
         ],
         compiler_params=pltpu.CompilerParams(
-            collective_id=0, has_side_effects=True, vmem_limit_bytes=60 * 1024 * 1024
+            collective_id=0, has_side_effects=True, vmem_limit_bytes=63 * 1024 * 1024
         ),
         name="equilibrate",
     )(

time: 153 us -> 132 us (0.86)
  Pallas kernels: 148 us -> 126 us
    pallas_call x1, Pallas kernels: 148 us -> 126 us  [per_device(): pl.pallas_call(kernel, out_shape=(jax.ShapeDtypeStruct((ATOMS // 128, 128...]
where the time goes in v3:
time: 132 us; the launch traced here: 131 us
  Pallas kernels  126 us (95%)
  local copies, waits for them, and re-layouts  4.33 us (3%)
    pallas_call x1, Pallas kernels, per_device(): pl.pallas_call(kernel, out_shape=(jax.ShapeDtypeStruct((ATOMS // 128, 128...  126 us
    unnamed x3, local copies, waits for them, and re-layouts  4.33 us

profile of v3, /device:TPU:1, one launch (start us, length us, event | category | flops | bytes accessed | tf_op | source)
XLA Modules:
  0.0 131.4 jit_solution(9816965546967397358)
XLA Ops:
  0.6 126.5 %equilibrate.1 = (f32[64,128]{1,0:T(8,128)}, f32[3,8192]{1,0:T(4,128)}, f32[64,128]{1,0:T(8,128)}) custom-call(f32[64,8192]{1,0:T(8,128)} %desc_ref.1, s32[1,8192]{1,0:T(1,128)} %bitcast.3, f32[3,8192]{1,0:T(4,128)} %offs1_ref.1, s32[3,8192]{1,0:T(4,128)} %base1_ref.1, f32[3]{0:T(128)} %hard_ref.1, f32[3,25,64]{2,1,0:T(8,128)} %wf_ref.1, ...), custom_call_target="tpu_custom_call" | custom-call | tf_op jit(solution)/shard_map/equilibrate/pallas_call | solution.py:617
  127.1 1.4 %copy.23 = f32[8192]{0:T(1024)} copy(f32[8192]{0:T(1024)} %bitcast.5) | data formatting | bytes 65536
  128.5 1.6 %copy.24 = f32[3,8192]{1,0:T(4,128)} copy(f32[3,8192]{1,0:T(4,128)} %get-tuple-element.13) | data formatting | bytes 196608
  130.1 1.4 %copy.25 = f32[8192]{0:T(1024)} copy(f32[8192]{0:T(1024)} %bitcast.4) | data formatting | bytes 65536

commit v4 on v3

--- a/solution.py
+++ b/solution.py
@@ -76,16 +76,12 @@
     return jnp.where(2.0 * number >= M, number - M, number)
 
 
-def peers_x(ix, iq):
+def peers_x(ix):
     return [(step, {GX: lax.rem(ix + step, 4)}, lax.rem(ix + step, 4)) for step in (2, 1, 3)]
 
 
 def peers_p(ip):
     return [(step, {PAX: lax.rem(ip + step, 8)}, lax.rem(ip + step, 8)) for step in (4, 3, 5, 2, 6, 1, 7)]
-
-
-def peers_q(iq):
-    return [(step, {QAX: lax.rem(iq + step, 8)}, lax.rem(iq + step, 8)) for step in (4, 3, 5, 2, 6, 1, 7)]
 
 
 def peers_xq(ix, iq):
@@ -151,21 +147,33 @@
 
 
 def kernel(
-    desc_ref, types1_ref, offs1_ref, base1_ref, hard_ref,
+    desc_hbm, types1_ref, offs1_ref, base1_ref, hard_ref,
     wf_ref, ws_ref, wo_ref, sf_ref, sc_ref, so_ref,
-    hx_ref, hxt_ref, hp_ref, hq_ref, hqt_ref, lanes_ref,
+    hx_hbm, hxt_hbm, hp_hbm, hq_hbm, hqt_hbm, lanes_ref,
     out_charges_ref, out_forces_ref, out_short_ref,
     w_ref, s_ref, mx_ref, mp_ref, mq_ref, bx_ref, sx_ref, sp_mask_ref, sq_mask_ref,
     a0_ref, a1_ref, b0_ref, b1_ref, acc_ref,
     ones_ref, sp_ref, sd_ref, r1_ref, k1_ref, r2_ref, x2_ref, m_ref, r3_ref, r3x_ref, green_ref,
     z3_ref, z3x_ref, r3b_ref, k3b_ref, m2b_ref, r2b_ref, v1_ref, r1b_ref, phi0_ref, phi_ref,
-    image_ref, p0_ref, d1_ref, t_ref, arx_ref, arp_ref, arq_ref, ars_ref,
+    image_ref, p0_ref, d1_ref, t_ref, arp_ref, arq_ref, ars_ref,
     types_ref, offs_ref, base_ref, chi_ref, charges_ref, pre_ref, n1_ref, n2_ref, n3_ref, tall_ref,
+    alpha_ref, first_ref, second_ref, last_ref, desc_ref, hx_ref, hxt_ref, hp_ref, hq_ref, hqt_ref, load,
     send, recv,
 ):
     ix, ip, iq = lax.axis_index(GX), lax.axis_index(PAX), lax.axis_index(QAX)
     mine = ix * 8 + iq
-    to_x, to_p, to_q, to_xq = peers_x(ix, iq), peers_p(ip), peers_q(iq), peers_xq(ix, iq)
+    to_x, to_p, to_xq = peers_x(ix), peers_p(ip), peers_xq(ix, iq)
+    loads = [
+        pltpu.make_async_copy(source, target, load.at[k])
+        for k, (source, target) in enumerate(
+            (
+                (desc_hbm, desc_ref), (hx_hbm, hx_ref), (hp_hbm, hp_ref), (hq_hbm, hq_ref),
+                (hqt_hbm, hqt_ref), (hxt_hbm, hxt_ref),
+            )
+        )
+    ]
+    for copy in loads:
+        copy.start()
     barrier = pltpu.get_barrier_semaphore()
     for _, where, _ in to_xq + to_p:
         pl.semaphore_signal(barrier, inc=1, device_id=where, device_id_type=MESH)
@@ -184,15 +192,24 @@
     n3_ref[...] = jnp.zeros(n3_ref.shape, F32)
     tall_ref[...] = jnp.zeros(tall_ref.shape, F32)
     for e in range(3):
-        n1_ref[32 * e : 32 * e + 25, :] = wf_ref[e]
-        n1_ref[96 + 32 * e : 96 + 32 * e + 25, :] = sf_ref[e]
+        n1_ref[32 * e : 32 * e + 25, 0:64] = wf_ref[e]
+        n1_ref[96 + 32 * e : 96 + 32 * e + 25, 0:64] = sf_ref[e]
         n2_ref[32 * e : 32 * e + 25, 0:25] = ws_ref[e]
     n3_ref[0:3, 0:25] = wo_ref[...]
-    n3_ref[8:11, 0:25] = so_ref[...]
+    n3_ref[16:19, 0:25] = so_ref[...]
     tall_ref[0:3, 0:25] = sc_ref[...]
     tall_ref[...] = jnp.transpose(tall_ref[...])
-    first_layer, second_layer = split(n1_ref[...]), split(n2_ref[...])
-    last_layer, short_layer = split(n3_ref[0:8, :]), split(n3_ref[8:16, :])
+    high, low = split(n1_ref[...])
+    high = high.astype(F32)
+    first_ref[:, 0:128] = (high + pltpu.roll(high, 64, 1)).astype(BF16)
+    first_ref[:, 128:256] = low
+    for source, stacked in ((n2_ref, second_ref), (n3_ref, last_ref)):
+        high, low = (half.astype(F32) for half in split(source[...]))
+        stacked[...] = (high + pltpu.roll(high, 32, 1) + pltpu.roll(low, 64, 1)).astype(BF16)
+
+    def layer(weights, value):
+        high, low = split(value)
+        return dot(weights, jnp.concatenate([high, low, high], axis=0))
 
     def wide(i):
         return pl.ds(i * WIDE, WIDE)
@@ -202,18 +219,18 @@
         return jnp.where(kind == 0, first, jnp.where(kind == 1, second, third))
 
     def net_chi(i, carry):
-        pre = dot3([half[0:96] for half in first_layer], desc_ref[:, wide(i)])
+        pre = layer(first_ref[0:96, 0:192], desc_ref[:, wide(i)])
         hidden = jnp.tanh(by_type(i, pre[0:32], pre[32:64], pre[64:96]))
-        pre = dot3(second_layer, hidden)
+        pre = layer(second_ref[:, 0:96], hidden)
         hidden = jnp.tanh(by_type(i, pre[0:32], pre[32:64], pre[64:96]))
-        value = dot3(last_layer, hidden)
+        value = layer(last_ref[0:16, 0:96], hidden)
         value = by_type(i, value[0:1], value[1:2], value[2:3])
         for k in range(WIDE // CH):
             chi_ref[pl.ds(WIDE // CH * i + k, 1), :] = value[:, CH * k : CH * k + CH]
         return carry
 
     def net_short(i, carry):
-        pre = dot3([half[96:192] for half in first_layer], desc_ref[:, wide(i)])
+        pre = layer(first_ref[96:192, 0:192], desc_ref[:, wide(i)])
         pre_ref[:, wide(i)] = by_type(i, pre[0:32], pre[32:64], pre[64:96])
         return carry
 
@@ -222,7 +239,7 @@
         charge = jnp.concatenate(rows, axis=1)
         weight = by_type(i, tall_ref[0:32, 0:1], tall_ref[0:32, 1:2], tall_ref[0:32, 2:3])
         hidden = jnp.tanh(pre_ref[:, wide(i)] + weight * charge)
-        value = dot3(short_layer, hidden)
+        value = layer(last_ref[16:32, 0:96], hidden)
         value = by_type(i, value[0:1], value[1:2], value[2:3])
         for k in range(WIDE // 128):
             row = pl.ds(WIDE // 128 * i + k, 1)
@@ -349,18 +366,16 @@
         return jnp.sum(jnp.sum(array, axis=0, keepdims=True), axis=1, keepdims=True)
 
     def ar_start(phase, tile):
-        peers, slots, me, base = (
-            (to_x, arx_ref, ix, 112), (to_p, arp_ref, ip, 116), (to_q, arq_ref, iq, 124)
-        )[phase]
+        peers, slots, me, base = ((to_p, arp_ref, ip, 112), (to_xq, arq_ref, mine, 120))[phase]
         slots[me] = tile
         ars_ref[phase] = tile
         return send_all(peers, lambda number: ars_ref.at[phase], slots.at[me], send, recv, base)
 
     def ar_done(phase, copies):
         wait_all(copies)
-        return jnp.sum((arx_ref, arp_ref, arq_ref)[phase][...], axis=0)
-
-    def solve(local_sums=None, during=()):
+        return jnp.sum((arp_ref, arq_ref)[phase][...], axis=0)
+
+    def solve(local_sums=None, during=(), finish=None):
         halves_of = [slice(0, 128), slice(128, 256)]
         to_wait = []
         for h, lanes in enumerate(halves_of):
@@ -423,6 +438,8 @@
             sums = ar_start(0, pack(local_sums(total(energy_density))))
         to_wait.append(copies)
         waits(copies)
+        if local_sums is not None:
+            sums = ar_start(1, ar_done(0, sums))
         rest = r3b_ref[comb(7), :]
         loaded = [
             jnp.concatenate([r3b_ref[comb(y), :], turn(rest, -16 * y)], axis=1) for y in range(7)
@@ -446,8 +463,6 @@
             moved.append(
                 send_all(to_p, lambda s: m2b_ref.at[h, s], r2b_ref.at[h, ip], send, recv, 88 + 8 * h)
             )
-        if local_sums is not None:
-            sums = ar_start(1, ar_done(0, sums))
         to_wait += moved
         back = []
         for h in range(2):
@@ -457,15 +472,14 @@
             back.append(
                 send_all(to_x, lambda g: v1_ref.at[h, g], r1b_ref.at[h, ix, 0:XR], send, recv, 104 + 4 * h)
             )
-        if local_sums is not None:
-            sums = ar_start(2, ar_done(1, sums))
         to_wait += back
+        if finish is not None:
+            finish(ar_done(1, sums))
         for copies in back:
             waits(copies)
         for copies in to_wait:
             for copy in copies:
                 copy.wait_send()
-        return None if local_sums is None else ar_done(2, sums)
 
     def field(g):
         return jnp.concatenate([r1b_ref[0, g], r1b_ref[1, g]], axis=1)
@@ -476,11 +490,11 @@
             both = jnp.concatenate([high.astype(F32), low.astype(F32)], axis=0)
             turned = jnp.transpose(both)[0:224, :].astype(BF16)
             phi_ref[224 * g : 224 * g + 224, 0:128] = turned
-            phi_ref[224 * g : 224 * g + 224, 128:256] = turned
+            phi_ref[224 * g : 224 * g + 224, 128:192] = turned[:, 0:64]
 
     def x_contract(table, c, slot):
         high, low = table[c, 0:64, :], table[c, 64:128, :]
-        t_ref[slot] = dot(phi_ref[...], jnp.concatenate([high, high, low, low], axis=0))
+        t_ref[slot] = dot(phi_ref[...], jnp.concatenate([high, high, low], axis=0))
 
     def fold(product):
         return (product[0:8] + product[8:16]) + (product[16:24] + product[24:32])
@@ -530,19 +544,19 @@
 
     atoms = float(ATOMS * 256)
     clear(256)
+    loads[0].wait()
     lax.fori_loop(0, ATOMS // WIDE, net_chi, 0)
     chi = chi_ref[...]
     local_sum = total(chi)
     shift = local_sum * (1.0 / ATOMS)
+    build(0, a0_ref, 0, b0_ref, chi_ref, shift)
+    spread_first(0, 2)
     pl.semaphore_wait(barrier, len(to_xq) + len(to_p))
     copies = ar_start(0, pack([local_sum]))
-    build(0, a0_ref, 0, b0_ref, chi_ref, shift)
-    spread_first(0, 2)
+    spread_first(2, 4)
     copies = ar_start(1, ar_done(0, copies))
-    spread_first(2, 6)
-    copies = ar_start(2, ar_done(1, copies))
-    spread_first(6, PAIRS)
-    mean = ar_done(2, copies)[0:1, 0:1] * (1.0 / atoms)
+    spread_first(4, PAIRS)
+    mean = ar_done(1, copies)[0:1, 0:1] * (1.0 / atoms)
     for g in range(4):
         turned = jnp.transpose(acc_ref[256 * g : 256 * g + 256, :])
         ones = turned[128:192] + turned[192:256]
@@ -552,6 +566,8 @@
         sd_ref[g] = density
     p0 = mean - chi
     p0_ref[...] = p0
+    for copy in loads[1:]:
+        copy.wait()
     solve(
         during=(
             lambda: lax.fori_loop(0, ATOMS // WIDE, net_short, 0),
@@ -569,12 +585,10 @@
     sums = pack([total(p0 * p0), total(p0 * image), image_sum, total(image * image), total(p0)])
     clear(128)
     copies = ar_start(0, sums)
-    spread_image(0, 2)
+    spread_image(0, 3)
     copies = ar_start(1, ar_done(0, copies))
-    spread_image(2, 6)
-    copies = ar_start(2, ar_done(1, copies))
-    spread_image(6, PAIRS)
-    sums = ar_done(2, copies)
+    spread_image(3, PAIRS)
+    sums = ar_done(1, copies)
     norm0, curve0, image_total, image_square, p0_total = (sums[0:1, k : k + 1] for k in range(5))
     alpha0 = norm0 / curve0
     image_mean = image_total * (1.0 / atoms)
@@ -594,13 +608,26 @@
             - alpha0 * (turned[0:64] + turned[64:128])
         )
     d1 = d1_ref[...]
-    sums = solve(lambda energy: [total(residual * residual), total(hardness * d1 * d1) + energy])
-    d1 = d1_ref[...]
-    alpha1 = sums[0:1, 0:1] / sums[0:1, 1:2]
-    charges_ref[...] = alpha0 * p0_ref[...] + alpha1 * d1
-    lax.fori_loop(0, ATOMS // WIDE, net_end, 0)
-    load_field(lambda g: alpha0 * phi0_ref[g] + alpha1 * field(g))
+    def finish(sums):
+        alpha1 = sums[0:1, 0:1] / sums[0:1, 1:2]
+        charges_ref[...] = alpha0 * p0_ref[...] + alpha1 * d1_ref[...]
+        for g in range(4):
+            phi0_ref[g] = alpha0 * phi0_ref[g]
+        alpha_ref[...] = jnp.zeros((8, 128), F32) + alpha1
+        lax.fori_loop(0, ATOMS // WIDE, net_end, 0)
+
+    solve(
+        lambda energy: [total(residual * residual), total(hardness * d1 * d1) + energy],
+        finish=finish,
+    )
+    alpha1 = alpha_ref[0:1, 0:1]
+    load_field(lambda g: phi0_ref[g] + alpha1 * field(g))
     sample_forces()
+
+
+def hand_over(*refs):
+    for source, target in zip(refs[:3], refs[3:]):
+        target[...] = source[...]
 
 
 def per_device(
@@ -610,18 +637,19 @@
     tabs = tables()
     vmem = pl.BlockSpec(memory_space=pltpu.VMEM)
     smem = pl.BlockSpec(memory_space=pltpu.SMEM)
+    far = pl.BlockSpec(memory_space=pl.ANY)
 
     def held(*shape, dtype=F32):
         return pltpu.VMEM(shape, dtype)
 
-    charges, forces, short_energy = pl.pallas_call(
+    results = pl.pallas_call(
         kernel,
         out_shape=(
             jax.ShapeDtypeStruct((ATOMS // 128, 128), F32),
             jax.ShapeDtypeStruct((3, ATOMS), F32),
             jax.ShapeDtypeStruct((ATOMS // 128, 128), F32),
         ),
-        in_specs=[vmem] * 4 + [smem] + [vmem] * 12,
+        in_specs=[far] + [vmem] * 3 + [smem] + [vmem] * 6 + [far] * 5 + [vmem],
         out_specs=(vmem, vmem, vmem),
         scratch_shapes=[
             held(3, 5, NCH, CH), held(3, 5, NCH, CH),
@@ -636,15 +664,19 @@
             held(256, LN), held(256, 128), held(256, 128), held(256, 128), held(M, LN),
             held(256, 128), held(256, 128), held(256, 128), held(256, LN),
             held(2, 8, 24, 128), held(2, 8, 24, 128), held(2, 4, XR, 128),
-            held(2, 4, 64, 128), held(4, 64, LN), held(896, 256, dtype=BF16),
+            held(2, 4, 64, 128), held(4, 64, LN), held(896, 192, dtype=BF16),
             held(NCH, CH), held(NCH, CH), held(NCH, CH),
             held(4, 896, CH),
-            held(4, 8, 128), held(8, 8, 128), held(8, 8, 128), held(3, 8, 128),
+            held(8, 8, 128), held(32, 8, 128), held(2, 8, 128),
             held(NCH, CH, dtype=jnp.int32), held(3, NCH, CH), held(3, NCH, CH, dtype=jnp.int32),
             held(NCH, CH), held(NCH, CH), held(32, ATOMS),
-            held(192, 64), held(96, 32), held(16, 32), held(128, 128),
-            pltpu.SemaphoreType.DMA((132,)),
-            pltpu.SemaphoreType.DMA((132,)),
+            held(192, 128), held(96, 128), held(32, 128), held(128, 128),
+            held(8, 128), held(192, 256, dtype=BF16), held(96, 128, dtype=BF16), held(32, 128, dtype=BF16),
+            held(64, ATOMS), held(2, M, 224, dtype=BF16), held(2, 224, M, dtype=BF16),
+            held(2, 256, 256, dtype=BF16), held(2, M, 256, dtype=BF16), held(2, 256, M, dtype=BF16),
+            pltpu.SemaphoreType.DMA((6,)),
+            pltpu.SemaphoreType.DMA((152,)),
+            pltpu.SemaphoreType.DMA((152,)),
         ],
         compiler_params=pltpu.CompilerParams(
             collective_id=0, has_side_effects=True, vmem_limit_bytes=63 * 1024 * 1024
@@ -655,6 +687,13 @@
         w_first, w_second, w_out, sr_first, sr_charge, sr_out,
         *[jnp.asarray(t) for t in tabs],
     )
+    charges, forces, short_energy = pl.pallas_call(
+        hand_over,
+        out_shape=tuple(jax.ShapeDtypeStruct(r.shape, F32) for r in results),
+        in_specs=[vmem] * 3,
+        out_specs=(vmem,) * 3,
+        name="hand_over",
+    )(*results)
     return charges.reshape(ATOMS), forces, short_energy.reshape(ATOMS)
 
 

time: 132 us -> 123 us (0.932)
  local copies, waits for them, and re-layouts: 4.33 us -> 0 us
  Pallas kernels: 126 us -> 123 us
    pallas_call x1, Pallas kernels: 126 us -> 121 us  [per_device(): pl.pallas_call(kernel, out_shape=(jax.ShapeDtypeStruct((ATOMS // 128, 128...]
    unnamed x3 -> x0, local copies, waits for them, and re-layouts: 4.33 us -> none
    pallas_call x0 -> x1, Pallas kernels: none -> 1.59 us  [per_device(): pl.pallas_call(hand_over, out_shape=tuple((jax.ShapeDtypeStruct(r.shape,...]
where the time goes in v4:
time: 123 us
  Pallas kernels  123 us (100%)
    pallas_call x1, Pallas kernels, per_device(): pl.pallas_call(kernel, out_shape=(jax.ShapeDtypeStruct((ATOMS // 128, 128...  121 us

profile of v4, /device:TPU:1, one launch (start us, length us, event | category | flops | bytes accessed | tf_op | source)
XLA Modules:
  0.0 123.3 jit_solution(529723974774776361)
XLA Ops:
  0.6 121.1 %equilibrate.1 = (f32[64,128]{1,0:T(8,128)}, f32[3,8192]{1,0:T(4,128)}, f32[64,128]{1,0:T(8,128)}) custom-call(f32[64,8192]{1,0:T(8,128)} %desc_hbm.1, s32[1,8192]{1,0:T(1,128)} %bitcast.3, f32[3,8192]{1,0:T(4,128)} %offs1_ref.1, s32[3,8192]{1,0:T(4,128)} %base1_ref.1, f32[3]{0:T(128)} %hard_ref.1, f32[3,25,64]{2,1,0:T(8,128)} %wf_ref.1, ...), custom_call_target="tpu_custom_call" | custom-call | tf_op jit(solution)/shard_map/equilibrate/pallas_call | solution.py:645
  121.7 1.6 %hand_over.1 = (f32[64,128]{1,0:T(8,128)}, f32[3,8192]{1,0:T(4,128)}, f32[64,128]{1,0:T(8,128)}) custom-call(f32[64,128]{1,0:T(8,128)} %get-tuple-element.9.refs_0_, f32[3,8192]{1,0:T(4,128)} %get-tuple-element.10.refs_1_, f32[64,128]{1,0:T(8,128)} %get-tuple-element.11.refs_2_), custom_call_target="tpu_custom_call" | custom-call | tf_op jit(solution)/shard_map/hand_over/pallas_call | solution.py:690

commit v5 on v4

--- a/solution.py
+++ b/solution.py
@@ -167,13 +167,18 @@
         pltpu.make_async_copy(source, target, load.at[k])
         for k, (source, target) in enumerate(
             (
-                (desc_hbm, desc_ref), (hx_hbm, hx_ref), (hp_hbm, hp_ref), (hq_hbm, hq_ref),
+                (hx_hbm, hx_ref), (hp_hbm, hp_ref), (hq_hbm, hq_ref),
                 (hqt_hbm, hqt_ref), (hxt_hbm, hxt_ref),
             )
         )
     ]
-    for copy in loads:
-        copy.start()
+
+    def piece(i):
+        lanes = pl.ds(i * WIDE, WIDE)
+        return pltpu.make_async_copy(desc_hbm.at[:, lanes], desc_ref.at[:, lanes], load.at[5 + i])
+
+    for i in range(ATOMS // WIDE):
+        piece(i).start()
     barrier = pltpu.get_barrier_semaphore()
     for _, where, _ in to_xq + to_p:
         pl.semaphore_signal(barrier, inc=1, device_id=where, device_id_type=MESH)
@@ -219,6 +224,7 @@
         return jnp.where(kind == 0, first, jnp.where(kind == 1, second, third))
 
     def net_chi(i, carry):
+        piece(i).wait()
         pre = layer(first_ref[0:96, 0:192], desc_ref[:, wide(i)])
         hidden = jnp.tanh(by_type(i, pre[0:32], pre[32:64], pre[64:96]))
         pre = layer(second_ref[:, 0:96], hidden)
@@ -273,24 +279,8 @@
         for j in range(5):
             w_ref[d, j] = spline[4 - j]
 
-    row = lax.broadcasted_iota(jnp.int32, (M, LN), 0).astype(F32)
-    f_q = signed(row)
-    f_p = signed(lanes_ref[0:1, :] + (6 * mine).astype(F32))
-    f_x = signed(lanes_ref[1:2, :] + (24 * ip).astype(F32))
-    factor = 2.0 * math.pi / M
-    wave = (factor * factor) * (f_q * f_q + (f_p * f_p + f_x * f_x))
-    safe = jnp.where(wave > 0, wave, 1.0)
-    green_ref[...] = jnp.where(
-        wave > 0, (4.0 * math.pi / (M * M * M)) * jnp.exp((-0.5 * SMEAR * SMEAR) * wave) / safe, 0.0
-    )
-
     for g in range(4):
-        for h in range(2):
-            r1b_ref[h, g, XR : XR + 8, :] = jnp.zeros((8, 128), F32)
         acc_ref[256 * g + 224 : 256 * g + 256, :] = jnp.zeros((32, 256), F32)
-    x2_ref[168:256, :] = jnp.zeros((88, LN), F32)
-    r3x_ref[comb(7), :] = jnp.zeros((32, 128), F32)
-    k3b_ref[192:256, :] = jnp.zeros((64, LN), F32)
 
     def mask(table, d, c, count):
         base = base_ref[d, pl.ds(c, 1), :]
@@ -344,8 +334,7 @@
                 b_ref[0:64, :], b_ref[64:128, :] = split(mx_ref[c] * value)
             part = dot(a0_ref[i], b0_ref[0:128, :], ((1,), (1,)))
             other = dot(a1_ref[i], b1_ref[0:128, :], ((1,), (1,)))
-            gather_part(part, 128)
-            gather_part(other, 128)
+            gather_part(part + other, 128)
             return carry
 
         lax.fori_loop(lo, hi, step, 0)
@@ -374,6 +363,25 @@
     def ar_done(phase, copies):
         wait_all(copies)
         return jnp.sum((arp_ref, arq_ref)[phase][...], axis=0)
+
+    def prepare():
+        row = lax.broadcasted_iota(jnp.int32, (M, LN), 0).astype(F32)
+        f_q = signed(row)
+        f_p = signed(lanes_ref[0:1, :] + (6 * mine).astype(F32))
+        f_x = signed(lanes_ref[1:2, :] + (24 * ip).astype(F32))
+        factor = 2.0 * math.pi / M
+        wave = (factor * factor) * (f_q * f_q + (f_p * f_p + f_x * f_x))
+        safe = jnp.where(wave > 0, wave, 1.0)
+        green_ref[...] = jnp.where(
+            wave > 0, (4.0 * math.pi / (M * M * M)) * jnp.exp((-0.5 * SMEAR * SMEAR) * wave) / safe, 0.0
+        )
+        for g in range(4):
+            for h in range(2):
+                r1b_ref[h, g, XR : XR + 8, :] = jnp.zeros((8, 128), F32)
+        x2_ref[...] = jnp.zeros((256, LN), F32)
+        r3x_ref[comb(7), :] = jnp.zeros((32, 128), F32)
+        k3b_ref[192:256, :] = jnp.zeros((64, LN), F32)
+        lax.fori_loop(0, ATOMS // WIDE, net_short, 0)
 
     def solve(local_sums=None, during=(), finish=None):
         halves_of = [slice(0, 128), slice(128, 256)]
@@ -400,16 +408,20 @@
             waits(moved[h])
             for y in range(4 * h, min(4 * h + 4, 7)):
                 for side in range(2):
-                    x2_ref[24 * y : 24 * y + 24, 128 * side : 128 * side + 128] = lane_pick(
+                    x2_ref[32 * y : 32 * y + 24, 128 * side : 128 * side + 128] = lane_pick(
                         [(r2_ref[h, 4 * side + s], 32 * (s - y)) for s in range(4)], 32
                     )
         k2 = dot3((hp_ref[0, 0:M, :], hp_ref[1, 0:M, :]), x2_ref[...], ((1,), (1,)))
         lane = lax.broadcasted_iota(jnp.int32, (32, 128), 1)
         rest = jnp.zeros((32, 128), F32)
         for y in range(7):
-            block = lane_pick([(k2[32 * k : 32 * k + 32, :], 24 * (k - y)) for k in range(6)], 24)
-            m_ref[comb(y), :] = block[:, 0:128]
-            rest = jnp.where((lane >= 16 * y) & (lane < 16 * y + 16), turn(block[:, 128:256], 16 * y), rest)
+            tile = k2[:, halves_of[y // 4]]
+            start = 32 * (y % 4)
+            m_ref[comb(y), :] = lane_pick(
+                [(tile[32 * k : 32 * k + 32], 24 * k - start) for k in range(6)], 24
+            )
+            inside = (lane >= 16 * y) & (lane < 16 * y + 16)
+            rest = jnp.where(inside, turn(tile[160:192], 120 - start + 16 * y), rest)
         m_ref[comb(7), :] = rest
         r3_ref[rows8(8 * mine), :] = m_ref[rows8(8 * mine), :]
         copies = send_all(
@@ -441,13 +453,17 @@
         if local_sums is not None:
             sums = ar_start(1, ar_done(0, sums))
         rest = r3b_ref[comb(7), :]
-        loaded = [
-            jnp.concatenate([r3b_ref[comb(y), :], turn(rest, -16 * y)], axis=1) for y in range(7)
-        ]
+        loaded = [r3b_ref[comb(y), :] for y in range(7)]
+        last = [jnp.where(lane >= 120, loaded[y], turn(rest, -16 * y)) for y in range(7)]
         for k in range(6):
-            k3b_ref[32 * k : 32 * k + 32, :] = lane_pick(
-                [(loaded[y], 24 * (y - k)) for y in range(7)], 24
-            )
+            for h in range(2):
+                k3b_ref[32 * k : 32 * k + 32, halves_of[h]] = lane_pick(
+                    [
+                        ((last if k == 5 else loaded)[y], 32 * (y % 4) - 24 * k)
+                        for y in range(4 * h, min(4 * h + 4, 7))
+                    ],
+                    32,
+                )
         turned = jnp.transpose(k3b_ref[...])
         high, low = split(turned)
         v2 = dot(high, hp_ref[0]) + (dot(low, hp_ref[0]) + dot(high, hp_ref[1]))
@@ -456,7 +472,7 @@
             for s in range(8):
                 lanes = halves_of[s // 4]
                 m2b_ref[h, s] = lane_pick(
-                    [(v2[24 * y : 24 * y + 24, lanes], 32 * (y - s)) for y in range(4 * h, min(4 * h + 4, 7))],
+                    [(v2[32 * y : 32 * y + 24, lanes], 32 * (y - s)) for y in range(4 * h, min(4 * h + 4, 7))],
                     32,
                 )
             r2b_ref[h, ip] = m2b_ref[h, ip]
@@ -544,8 +560,9 @@
 
     atoms = float(ATOMS * 256)
     clear(256)
-    loads[0].wait()
     lax.fori_loop(0, ATOMS // WIDE, net_chi, 0)
+    for copy in loads:
+        copy.start()
     chi = chi_ref[...]
     local_sum = total(chi)
     shift = local_sum * (1.0 / ATOMS)
@@ -566,11 +583,11 @@
         sd_ref[g] = density
     p0 = mean - chi
     p0_ref[...] = p0
-    for copy in loads[1:]:
+    for copy in loads:
         copy.wait()
     solve(
         during=(
-            lambda: lax.fori_loop(0, ATOMS // WIDE, net_short, 0),
+            prepare,
             lambda: lax.fori_loop(0, NCH, slope_masks, 0),
         )
     )
@@ -674,7 +691,7 @@
             held(8, 128), held(192, 256, dtype=BF16), held(96, 128, dtype=BF16), held(32, 128, dtype=BF16),
             held(64, ATOMS), held(2, M, 224, dtype=BF16), held(2, 224, M, dtype=BF16),
             held(2, 256, 256, dtype=BF16), held(2, M, 256, dtype=BF16), held(2, 256, M, dtype=BF16),
-            pltpu.SemaphoreType.DMA((6,)),
+            pltpu.SemaphoreType.DMA((9,)),
             pltpu.SemaphoreType.DMA((152,)),
             pltpu.SemaphoreType.DMA((152,)),
         ],

time: 123 us -> 123 us (level)
  no operation moved by 1% of the time
where the time goes in v5:
time: 123 us; the launch traced here: 122 us
  Pallas kernels  122 us (99%)
    pallas_call x1, Pallas kernels, per_device(): pl.pallas_call(kernel, out_shape=(jax.ShapeDtypeStruct((ATOMS // 128, 128...  120 us

profile of v5, /device:TPU:1, one launch (start us, length us, event | category | flops | bytes accessed | tf_op | source)
XLA Modules:
  0.0 122.4 jit_solution(7377286026490349491)
XLA Ops:
  0.6 120.1 %equilibrate.1 = (f32[64,128]{1,0:T(8,128)}, f32[3,8192]{1,0:T(4,128)}, f32[64,128]{1,0:T(8,128)}) custom-call(f32[64,8192]{1,0:T(8,128)} %desc_hbm.1, s32[1,8192]{1,0:T(1,128)} %bitcast.3, f32[3,8192]{1,0:T(4,128)} %offs1_ref.1, s32[3,8192]{1,0:T(4,128)} %base1_ref.1, f32[3]{0:T(128)} %hard_ref.1, f32[3,25,64]{2,1,0:T(8,128)} %wf_ref.1, ...), custom_call_target="tpu_custom_call" | custom-call | tf_op jit(solution)/shard_map/equilibrate/pallas_call | solution.py:662
  120.8 1.6 %hand_over.1 = (f32[64,128]{1,0:T(8,128)}, f32[3,8192]{1,0:T(4,128)}, f32[64,128]{1,0:T(8,128)}) custom-call(f32[64,128]{1,0:T(8,128)} %get-tuple-element.9.refs_0_, f32[3,8192]{1,0:T(4,128)} %get-tuple-element.10.refs_1_, f32[64,128]{1,0:T(8,128)} %get-tuple-element.11.refs_2_), custom_call_target="tpu_custom_call" | custom-call | tf_op jit(solution)/shard_map/hand_over/pallas_call | solution.py:707
